TPU v7x, 8 devices: a whole 2x2x1 slice. The times are simulated.
8 devices in a mesh: dp: 1 (over z), tp: 8 (over y, x, core).
Axes of the slice: x: 2, y: 2, z: 1, core: 2. Of those that a mesh axis runs over, the one named last changes fastest.
Arguments:
- x: bfloat16 [256, 2048], P('dp')
- ln_attn_gamma: float32 [2048], replicated
- ln_attn_beta: float32 [2048], replicated
- ln_mlp_gamma: float32 [2048], replicated
- ln_mlp_beta: float32 [2048], replicated
- w_qkv: bfloat16 [2048, 16, 3, 128], P(None, 'tp')
- w_out: bfloat16 [16, 1, 128, 2048], P('tp')
- w_up: bfloat16 [2048, 8192], P(None, 'tp')
- w_down: bfloat16 [8192, 2048], P('tp')
- k_cache: bfloat16 [256, 16, 128, 128], P('dp', 'tp')
- v_cache: bfloat16 [256, 16, 128, 128], P('dp', 'tp')
- positions: int32 [256], P('dp')
Outputs:
- output 1: bfloat16 [256, 2048], P('dp')
- output 2: bfloat16 [256, 16, 128, 128], P('dp', 'tp')
- output 3: bfloat16 [256, 16, 128, 128], P('dp', 'tp')
All inputs are finite; a program needn't handle non-finite values.
Results may differ from a plain program's by a relative error of at most 0.0110546.
Values are sent between devices in bfloat16 or wider.
A program may use at most 1 GiB of HBM per device.

v0:
```python
import jax
import jax.numpy as jnp
from jax import lax
from jax.sharding import PartitionSpec as P

LN_EPS = 1e-5
ROPE_BASE = 10000.0
NEG_BIG = -1e30


def layer_norm(act_rows, ln_gamma, ln_beta):
    rows_f32 = act_rows.astype(jnp.float32)
    row_mean = jnp.mean(rows_f32, axis=-1, keepdims=True)
    centred = rows_f32 - row_mean
    row_var = jnp.mean(centred * centred, axis=-1, keepdims=True)
    return (centred * lax.rsqrt(row_var + LN_EPS) * ln_gamma + ln_beta).astype(jnp.bfloat16)


def apply_rotary(vectors, cos_t, sin_t):
    half_width = vectors.shape[-1] // 2
    as_f32 = vectors.astype(jnp.float32)
    lower_half = as_f32[..., :half_width]
    upper_half = as_f32[..., half_width:]
    return jnp.concatenate([lower_half * cos_t - upper_half * sin_t, upper_half * cos_t + lower_half * sin_t], axis=-1).astype(jnp.bfloat16)


def attend_local(attn_in, w_qkv, k_cache, v_cache, positions):
    n_query = w_qkv.shape[2] - 2
    head_dim = w_qkv.shape[3]
    qkv_rows = jnp.einsum('bd,dgjh->bgjh', attn_in, w_qkv, preferred_element_type=jnp.float32).astype(jnp.bfloat16)
    inv_freq = ROPE_BASE ** (-2.0 * jnp.arange(head_dim // 2, dtype=jnp.float32) / head_dim)
    angles = positions.astype(jnp.float32)[:, None] * inv_freq[None, :]
    cos_t = jnp.cos(angles)
    sin_t = jnp.sin(angles)
    queries = apply_rotary(qkv_rows[:, :, :n_query], cos_t[:, None, None, :], sin_t[:, None, None, :])
    new_key = apply_rotary(qkv_rows[:, :, n_query], cos_t[:, None, :], sin_t[:, None, :])
    new_value = qkv_rows[:, :, n_query + 1]
    slot_ids = jnp.arange(k_cache.shape[2])
    write_mask = (slot_ids[None, :] == positions[:, None])[:, None, :, None]
    keys_all = jnp.where(write_mask, new_key[:, :, None, :], k_cache)
    values_all = jnp.where(write_mask, new_value[:, :, None, :], v_cache)
    valid_mask = (slot_ids[None, :] <= positions[:, None])[:, None, None, :]
    scores = jnp.einsum('bgqh,bgsh->bgqs', queries, keys_all, preferred_element_type=jnp.float32) * (head_dim ** -0.5)
    scores = jnp.where(valid_mask, scores, NEG_BIG)
    attn_probs = jax.nn.softmax(scores, axis=-1).astype(jnp.bfloat16)
    context = jnp.einsum('bgqs,bgsh->bgqh', attn_probs, values_all, preferred_element_type=jnp.float32).astype(jnp.bfloat16)
    return context, keys_all, values_all


def solution(mesh):
    row_spec = P('dp', None)
    vec_spec = P(None)
    cache_spec = P('dp', 'tp', None, None)

    def device_step(x, ln_attn_gamma, ln_attn_beta, ln_mlp_gamma, ln_mlp_beta, w_qkv, w_out, w_up, w_down, k_cache, v_cache, positions):
        attn_in = layer_norm(x, ln_attn_gamma, ln_attn_beta)
        mlp_in = layer_norm(x, ln_mlp_gamma, ln_mlp_beta)
        context, keys_all, values_all = attend_local(attn_in, w_qkv, k_cache, v_cache, positions)
        attn_part = jnp.einsum('bgqh,gqhd->bd', context, w_out, preferred_element_type=jnp.float32).astype(jnp.bfloat16)
        attn_total = lax.psum(attn_part, 'tp')
        hidden = jax.nn.gelu(jnp.dot(mlp_in, w_up, preferred_element_type=jnp.float32), approximate=False).astype(jnp.bfloat16)
        mlp_part = jnp.dot(hidden, w_down, preferred_element_type=jnp.float32).astype(jnp.bfloat16)
        mlp_total = lax.psum(mlp_part, 'tp')
        layer_out = (x.astype(jnp.float32) + attn_total.astype(jnp.float32) + mlp_total.astype(jnp.float32)).astype(jnp.bfloat16)
        return layer_out, keys_all, values_all

    return jax.shard_map(device_step, mesh=mesh, in_specs=(row_spec, vec_spec, vec_spec, vec_spec, vec_spec, P(None, 'tp', None, None), P('tp', None, None, None), P(None, 'tp'), P('tp', None), cache_spec, cache_spec, P('dp')), out_specs=(row_spec, cache_spec, cache_spec), check_vma=False)
```

profile of v0, /device:TPU:0, one launch (start us, length us, event | category | flops | bytes accessed | tf_op | source)
XLA Modules:
  0.0 141.9 jit_solution(14316568610602093713)
XLA Ops:
  7.2 0.0 copy-start
  7.2 0.0 all-reduce.3.cloned.1.call-start
  7.2 0.8 convert_element_type.65
  8.0 0.8 iota_compare_fusion.1
  8.8 1.4 %convert_reduce_fusion = f32[256]{0:T(256)S(1)} fusion(bf16[256,2048]{1,0:T(8,128)(2,1)} %param.12), kind=kLoop, calls=%fused_computation.6 | loop fusion | flops 1048320 | bytes 1049600 | tf_op jit(solution)/shard_map/reduce_sum | solution.py:13
  10.2 1.6 %fusion.11 = f32[256]{0:T(256)S(1)} fusion(bf16[256,2048]{1,0:T(8,128)(2,1)} %param.12, f32[256]{0:T(256)S(1)} %broadcast_multiply_fusion), kind=kLoop, calls=%fused_computation.18 | loop fusion | flops 2096896 | bytes 1050624 | tf_op jit(solution)/shard_map/reduce_sum | solution.py:15
  11.9 0.0 copy-start.1
  11.9 0.0 copy-start.2
  11.9 0.0 copy-start.3
  11.9 8.7 %copy.22 = bf16[2048,2,3,128]{0,3,2,1:T(8,128)(2,1)} copy(bf16[2048,2,3,128]{3,1,2,0:T(2,128)(2,1)} %param.17) | data formatting | bytes 6291456 | tf_op args[5]
  20.7 0.0 copy-done.1
  20.7 0.0 copy-done.2
  20.7 0.0 copy-done.3
  20.7 3.0 %fusion.24 = f32[256,768]{0,1:S(1)} fusion(bf16[2048,768]{0,1:T(8,128)(2,1)} %bitcast.64, bf16[256,2048]{1,0:T(8,128)(2,1)S(1)} %copy-done.1, f32[2048]{0:T(1024)S(1)} %copy-done.2, f32[2048]{0:T(1024)S(1)} %copy-done.3, f32[256]{0:T(256)S(1)} %add_rsqrt_fusion, f32[256]{0:T(256)S(1)} %broadcast_multiply_fusion), kind=kOutput, calls=%fused_computation.31 | convolution fusion | flops 808452096 | bytes 4999168
  23.8 0.1 fusion.81
  23.8 0.3 multiply_cosine_fusion
  24.3 0.1 copy.27
  24.4 0.2 copy.29
  24.6 0.1 copy.28
  24.7 23.0 %broadcast_select_fusion.1 = (bf16[256,2,128,128]{3,2,1,0:T(8,128)(2,1)}, bf16[256,2,128,128]{3,2,1,0:T(8,128)(2,1)}) fusion(bf16[256,2,128,128]{3,2,1,0:T(8,128)(2,1)} %param.21, pred[256,128]{1,0:T(8,128)(4,1)S(1)} %get-tuple-element.16, bf16[256,2,128]{2,1,0:T(2,128)(2,1)S(1)} %copy.27, bf16[256,2,128,128]{3,2,1,0:T(8,128)(2,1)} %param.22, ...), kind=kLoop, calls=%fused_computation.3 | loop fusion | flops 16777216 | bytes 67403776 | tf_op jit(solution)/shard_map/jit(_where)/select_n | solution.py:40
  47.8 12.2 %fusion.130 = f32[256,2,1,128]{3,2,1,0:T(1,128)S(1)} fusion(bf16[256,2,128,1]{2,3,1,0:T(2,128)(2,1)S(1)} %copy.29, bf16[256,2,128,128]{3,2,1,0:T(8,128)(2,1)} %get-tuple-element.11), kind=kOutput, calls=%fused_computation.154 | convolution fusion | flops 16777216 | bytes 17170432 | tf_op jit(solution)/shard_map/bgqh,bgsh->bgqs/dot_general | solution.py:43
  60.0 0.3 fusion.18
  60.2 0.0 copy-start.4
  60.3 0.0 copy-start.5
  60.3 8.1 %fusion.77 = bf16[256,2,1,128]{3,2,1,0:T(2,128)(2,1)S(1)} fusion(bf16[256,2,128,128]{3,2,1,0:T(8,128)(2,1)} %get-tuple-element.12, bf16[256,2,128,1]{2,0,1,3:T(8,128)(2,1)S(1)} %fusion.18), kind=kOutput, calls=%fused_computation.89 | convolution fusion | flops 16777216 | bytes 17039360 | tf_op jit(solution)/shard_map/bgqs,bgsh->bgqh/dot_general | solution.py:46
  68.3 0.0 copy-done
  68.3 1.4 %fusion.2 = bf16[256,2048]{1,0:T(8,128)(2,1)} fusion(bf16[2,1,128,2048]{3,2,1,0:T(8,128)(2,1)S(1)} %copy-done, bf16[256,2,1,128]{3,2,1,0:T(2,128)(2,1)S(1)} %fusion.77), kind=kOutput, calls=%fused_computation.8 | convolution fusion | flops 268959744 | bytes 2228224 | tf_op jit(solution)/shard_map/bgqh,gqhd->bd/dot_general | solution.py:59
  69.8 0.0 copy-done.4
  69.8 0.0 copy-done.5
  69.8 9.0 %convolution_convert_fusion = bf16[256,2048]{1,0:T(8,128)(2,1)} fusion(bf16[1024,2048]{1,0:T(8,128)(2,1)} %param.20, bf16[2048,1024]{1,0:T(8,128)(2,1)} %param.19, bf16[256,2048]{1,0:T(8,128)(2,1)S(1)} %copy-done.1, f32[2048]{0:T(1024)S(1)} %copy-done.4, f32[2048]{0:T(1024)S(1)} %copy-done.5, f32[256]{0:T(256)S(1)} %add_rsqrt_fusion, ...), kind=kOutput, calls=%fused_computation.9 | convolution fusion | flops 2168193024 | bytes 10504192 | tf_op jit(solution)/shard_map/dot_general | solution.py:62
  78.8 0.0 all-reduce.3.cloned.1.call-update
  78.8 53.1 %all-reduce.3.cloned.1.call-done = (bf16[256,2048]{1,0:T(8,128)(2,1)}, bf16[256,2048]{1,0:T(8,128)(2,1)}) async-done(((bf16[256,2048]{1,0:T(8,128)(2,1)}, bf16[256,2048]{1,0:T(8,128)(2,1)}), (bf16[256,2048]{1,0:T(8,128)(2,1)}, bf16[256,2048]{1,0:T(8,128)(2,1)})) %all-reduce.3.cloned.1.call-update) | async-done | bytes 2097168 | tf_op jit(solution)/shard_map/psum | solution.py:63
  132.0 3.1 %fusion.13 = bf16[256,2048]{1,0:T(8,128)(2,1)} fusion(bf16[256,2048]{1,0:T(8,128)(2,1)S(1)} %copy-done.1, bf16[256,2048]{1,0:T(8,128)(2,1)} %get-tuple-element.3, bf16[256,2048]{1,0:T(8,128)(2,1)} %get-tuple-element.4), kind=kLoop, calls=%fused_computation.20 | loop fusion | flops 3145728 | bytes 4194304 | tf_op jit(solution)/shard_map/convert_element_type | solution.py:64
  (9 shorter events, 0.2 us)
Async XLA Ops:
  7.2 61.2 %copy-start = (bf16[2,1,128,2048]{3,2,1,0:T(8,128)(2,1)S(1)}, bf16[2,1,128,2048]{3,2,1,0:T(8,128)(2,1)}, u32[]{:S(2)}) copy-start(bf16[2,1,128,2048]{3,2,1,0:T(8,128)(2,1)} %param.18) | copy-start | bytes 3145732
  7.2 124.8 %all-reduce.3.cloned.1.call-start = ((), (), s32[]{:S(2)}) async-start(), calls=%async_computation | async-start | bytes 4194304 | tf_op jit(solution)/shard_map/psum | solution.py:63
  11.9 8.8 %copy-start.1 = (bf16[256,2048]{1,0:T(8,128)(2,1)S(1)}, bf16[256,2048]{1,0:T(8,128)(2,1)}, u32[]{:S(2)}) copy-start(bf16[256,2048]{1,0:T(8,128)(2,1)} %param.12) | copy-start | bytes 3145732
  11.9 8.7 %copy-start.2 = (f32[2048]{0:T(1024)S(1)}, f32[2048]{0:T(1024)}, u32[]{:S(2)}) copy-start(f32[2048]{0:T(1024)} %param.14) | copy-start | bytes 24580
  11.9 8.7 %copy-start.3 = (f32[2048]{0:T(1024)S(1)}, f32[2048]{0:T(1024)}, u32[]{:S(2)}) copy-start(f32[2048]{0:T(1024)} %param.13) | copy-start | bytes 24580
  60.2 9.5 %copy-start.4 = (f32[2048]{0:T(1024)S(1)}, f32[2048]{0:T(1024)}, u32[]{:S(2)}) copy-start(f32[2048]{0:T(1024)} %param.16) | copy-start | bytes 24580
  60.3 9.5 %copy-start.5 = (f32[2048]{0:T(1024)S(1)}, f32[2048]{0:T(1024)}, u32[]{:S(2)}) copy-start(f32[2048]{0:T(1024)} %param.15) | copy-start | bytes 24580
Sparse Core Ops, SparseCore 0:
  79.0 52.9 all-reduce.2
where the time goes:
time: 142 us
  waiting for transfers between devices  53.1 us (37%)
  matrix products  33.8 us (24%)
  other arithmetic  31.5 us (22%)
  between operations  14.2 us (10%)
  local copies, waits for them, and re-layouts  9.15 us (6%)
    psum x1, waiting for transfers between devices, device_step(): mlp_total = lax.psum(mlp_part, 'tp')  53.1 us
    select_n x1, other arithmetic, attend_local(): keys_all = jnp.where(write_mask, new_key[:, :, None, :], k_cache)  23 us
    dot_general x1, matrix products, attend_local(): jnp.einsum('bgqh,bgsh->bgqs', queries, keys_all, preferred_element_type=j...  12.2 us
    dot_general x1, matrix products, device_step(): jnp.dot(hidden, w_down, preferred_element_type=jnp.float32)  9.03 us
    unnamed x13, local copies, waits for them, and re-layouts  8.76 us
    dot_general x1, matrix products, attend_local(): jnp.einsum('bgqs,bgsh->bgqh', attn_probs, values_all, preferred_element_t...  8.06 us
    convert_element_type x1, other arithmetic, device_step(): (x.astype(jnp.float32) + attn_total.astype(jnp.float32) + mlp_total.astyp...  3.05 us
    unnamed x1, matrix products  3.04 us
  transfers between devices with their start and end apart: 1, of which 1 were waited for; matrix products, arithmetic and copies ran while one was open for 0% of the time, Pallas kernels for 0%

commit v1 on v0

v1 whole, which is shorter than its diff:
```python
import functools
import math

import jax
import jax.numpy as jnp
from jax import lax
from jax.experimental import pallas as pl
from jax.experimental.pallas import tpu as pltpu
from jax.sharding import PartitionSpec as P

LN_EPS = 1e-5
ROPE_BASE = 10000.0
NEG_BIG = -1e30
MESH = pl.DeviceIdType.MESH
F32 = jnp.float32
BF16 = jnp.bfloat16

B = 256
D = 2048
S = 128
H = 128
G = 2
FL = 1024
R0 = 64
CH = 64
NG = 16
SCALE = H ** -0.5


def dot(a, b):
    return jnp.dot(a, b, preferred_element_type=F32)


def iota(shape, dim):
    return lax.broadcasted_iota(jnp.int32, shape, dim)


def build_queries(q_ref, row, qt_ref):
    stacked = jnp.concatenate([q_ref[pl.ds(row, CH), pl.ds(0, H)], q_ref[pl.ds(row, CH), pl.ds(H, H)]], axis=0)
    turned = stacked.T
    low = iota((H, 2 * CH), 1) < CH
    qt_ref[pl.ds(0, H), :] = jnp.where(low, turned, 0.0).astype(BF16)
    qt_ref[pl.ds(H, H), :] = jnp.where(low, 0.0, turned).astype(BF16)


def slot_mask(pos_s, row, slots):
    at = jnp.full((S, H), pos_s[row].astype(F32), F32).astype(BF16)
    return slots == at


def new_rows(new_ref, row):
    rows = pl.ds(row if isinstance(row, int) else pl.multiple_of(row, NG), NG)
    return [new_ref[rows, pl.ds(g * H, H)] for g in range(G)]


def patched(cache, mask, new, u):
    return jnp.where(mask, jnp.broadcast_to(new[u:u + 1], (S, H)).astype(BF16), cache)


def scores_of_group(pos_s, kn_ref, kbuf, qt_ref, acc, row, at, local):
    slots = iota((S, H), 0).astype(F32).astype(BF16)
    lane = iota((S, 2 * CH), 1) & (CH - 1)
    new = new_rows(kn_ref, row)
    for u in range(NG):
        mask = slot_mask(pos_s, row + u, slots)
        halves = []
        for g in range(G):
            k = patched(kbuf[at + u, g], mask, new[g], u)
            kbuf[at + u, g] = k
            halves.append(k)
        full = dot(jnp.concatenate(halves, axis=1), qt_ref[...])
        acc = jnp.where(lane == local + u, full, acc)
    return acc


def softmax_slots(acc, pos_v, chunk):
    row = pos_v[pl.ds(chunk // 2, 1), :]
    lane = iota((1, 2 * CH), 1)
    turned = pltpu.roll(row, CH, 1)
    at = jnp.where(lane < CH, row, turned) if chunk % 2 == 0 else jnp.where(lane < CH, turned, row)
    s = jnp.where(iota((S, 2 * CH), 0) <= at, acc * SCALE, NEG_BIG)
    e = jnp.exp(s - jnp.max(s, axis=0, keepdims=True))
    p = e / jnp.sum(e, axis=0, keepdims=True)
    return p.T.astype(BF16)


def context_of_group(pos_s, vn_ref, vbuf, p_ref, ctx_ref, row, at, local):
    slots = iota((S, H), 0).astype(F32).astype(BF16)
    rows16 = iota((NG, S), 0).astype(F32).astype(BF16)
    new = new_rows(vn_ref, row)
    total = [None, None]
    probs = [p_ref[pl.ds(pl.multiple_of(g * CH + local, NG), NG), :] for g in range(G)]
    zero = jnp.zeros((NG, S), BF16)
    for u in range(0, NG, 2):
        masks = [slot_mask(pos_s, row + u + w, slots) for w in range(2)]
        for g in range(G):
            vs, ps = [], []
            for w in range(2):
                v = patched(vbuf[at + u + w, g], masks[w], new[g], u + w)
                vbuf[at + u + w, g] = v
                vs.append(v)
                ps.append(jnp.where(rows16 == jnp.asarray(u + w, BF16), probs[g], zero))
            part = dot(jnp.concatenate(ps, axis=1), jnp.concatenate(vs, axis=0))
            total[g] = part if total[g] is None else total[g] + part
    for g in range(G):
        ctx_ref[pl.ds(pl.multiple_of(local, NG), NG), pl.ds(g * H, H)] = total[g].astype(BF16)


def local_kernel(x_h, ga_h, ba_h, gm_h, bm_h, wq_h, wo_h, wu_h, wd_h, k_h, v_h, pos_s, pos_h,
                 ko_h, vo_h, q_o, kn_o, vn_o, m_o, part_o,
                 x_v, ln_v, wq_v, w32_v, wqb_v, wo_v, wu_v, wd_v, kb, vb, pos_v, ain_v, min_v, cos_v, sin_v, h_v, qt_v, p_v, ctx_v, a_v,
                 sem_in, sem_k, sem_v, sem_ko, sem_vo):
    ngr = R0 // NG

    def rd(src, dst, i):
        c = pltpu.make_async_copy(src, dst, sem_in.at[i])
        c.start()
        return c

    c_pos = rd(pos_h, pos_v, 0)
    c_x = rd(x_h, x_v, 1)
    c_ln = [rd(r, ln_v.at[pl.ds(8 * i, 1)], 2 + i) for i, r in enumerate((ga_h, ba_h, gm_h, bm_h))]
    c_wq = [rd(wq_h.at[pl.ds(3072 * i, 3072)], wq_v.at[pl.ds(3072 * i, 3072)], 6 + i) for i in range(4)]

    def kcopy(i, a, b, sem):
        return pltpu.make_async_copy(a.at[pl.ds(NG * i, NG)], b.at[pl.ds(NG * i, NG)], sem.at[i])

    for i in range(ngr):
        kcopy(i, k_h, kb, sem_k).start()
    for i in range(ngr):
        kcopy(i, v_h, vb, sem_v).start()
    c_wo = rd(wo_h, wo_v, 10)
    c_wu = [rd(wu_h.at[pl.ds(1024 * i, 1024)], wu_v.at[pl.ds(1024 * i, 1024)], 11 + i) for i in range(2)]
    c_wd = [rd(wd_h.at[pl.ds(512 * i, 512)], wd_v.at[pl.ds(512 * i, 512)], 13 + i) for i in range(2)]

    c_pos.wait()
    lane = iota((S, H), 1)
    inv = jnp.exp((lane & (H // 2 - 1)).astype(F32) * (-2.0 * math.log(ROPE_BASE) / H))
    for i in range(2):
        at = jnp.broadcast_to(pos_v[pl.ds(i, 1), :].astype(F32), (S, H)).T
        ang = at * inv
        sn = jnp.sin(ang)
        cos_v[pl.ds(S * i, S), :] = jnp.cos(ang)
        sin_v[pl.ds(S * i, S), :] = jnp.where(lane < H // 2, -sn, sn)

    c_x.wait()
    for c in c_ln:
        c.wait()
    RB = 32

    @pl.loop(0, B // RB)
    def _(i):
        r = pl.ds(pl.multiple_of(i * RB, RB), RB)

        def tile(j):
            return x_v[r, pl.ds(128 * j, 128)].astype(F32)

        tot = tile(0)
        for j in range(1, 16):
            tot = tot + tile(j)
        mean = jnp.sum(tot, axis=-1, keepdims=True) * (1.0 / D)
        tot = jnp.zeros((RB, 128), F32)
        for j in range(16):
            d = tile(j) - mean
            tot = tot + d * d
        rs = lax.rsqrt(jnp.sum(tot, axis=-1, keepdims=True) * (1.0 / D) + LN_EPS)
        for j in range(16):
            cs = pl.ds(128 * j, 128)
            n = (tile(j) - mean) * rs
            ain_v[r, cs] = (n * ln_v[pl.ds(0, 1), cs] + ln_v[pl.ds(8, 1), cs]).astype(BF16)
            min_v[r, cs] = (n * ln_v[pl.ds(16, 1), cs] + ln_v[pl.ds(24, 1), cs]).astype(BF16)

    for c in c_wq:
        c.wait()

    @pl.loop(0, 16)
    def _(i):
        w32_v[...] = wq_v[pl.ds(pl.multiple_of(i * 768, 768), 768), :].astype(F32)
        for j in range(3):
            for g in range(G):
                wqb_v[pl.ds(pl.multiple_of(i * 128, 128), 128), pl.ds((g * 3 + j) * H, H)] = (
                    w32_v[pl.ds(2 * j + g, 128, stride=6), :].astype(BF16))

    def rotary(u, r):
        return u * cos_v[r, :] + pltpu.roll(u, H // 2, 1) * sin_v[r, :]

    for n in range(3):
        qkv = dot(ain_v[...], wqb_v[:, pl.ds(256 * n, 256)]).astype(BF16).astype(F32)
        for w in range(2):
            g, j = divmod(2 * n + w, 3)
            u = qkv[:, w * H:(w + 1) * H]
            dst = (q_o, kn_o, vn_o)[j]
            if j < 2:
                u = rotary(u, pl.ds(0, B)).astype(BF16).astype(F32)
            dst[:, pl.ds(g * H, H)] = u

    for c in range(R0 // CH):
        build_queries(q_o, c * CH, qt_v)
        acc = jnp.zeros((S, 2 * CH), F32)

        def score_step(j, acc, c=c):
            i = c * (CH // NG) + j
            kcopy(i, k_h, kb, sem_k).wait()
            return scores_of_group(pos_s, kn_o, kb, qt_v, acc, i * NG, i * NG, j * NG)

        acc = lax.fori_loop(0, CH // NG, score_step, acc)
        p_v[...] = softmax_slots(acc, pos_v, c)
        for j in range(CH // NG):
            kcopy(c * (CH // NG) + j, kb, ko_h, sem_ko).start()

        @pl.loop(0, CH // NG)
        def _(j, c=c):
            i = c * (CH // NG) + j
            kcopy(i, v_h, vb, sem_v).wait()
            context_of_group(pos_s, vn_o, vb, p_v, ctx_v, i * NG, i * NG, j * NG)

        if c == 0:
            c_wo.wait()
        for n in range(8):
            a_v[pl.ds(c * CH, CH), pl.ds(256 * n, 256)] = dot(ctx_v[...], wo_v[:, pl.ds(256 * n, 256)])
        for j in range(CH // NG):
            kcopy(c * (CH // NG) + j, vb, vo_h, sem_vo).start()

    for c in c_wu:
        c.wait()
    for n in range(4):
        u = dot(min_v[...], wu_v[:, pl.ds(256 * n, 256)])
        h_v[:, pl.ds(256 * n, 256)] = (0.5 * u * (1.0 + lax.erf(u * (2.0 ** -0.5)))).astype(BF16)
    for c in c_wd:
        c.wait()
    for n in range(8):
        cs = pl.ds(256 * n, 256)
        m_o[:, cs] = dot(h_v[...], wd_v[:, cs])
        part_o[:, cs] = (a_v[:, cs] + m_o[pl.ds(0, R0), cs]).astype(BF16)

    for i in range(ngr):
        kcopy(i, kb, ko_h, sem_ko).wait()
        kcopy(i, vb, vo_h, sem_vo).wait()


def reduce_kernel(x_h, wo_h, k_h, v_h, q_i, kn_i, vn_i, m_i, part_i, pos_s, pos_i,
                  k2, v2, out_o,
                  x_v, wo_v, qt_v, p_v, ctx_v, part_v, d2_v, sum_v, rs_v, gat_v,
                  sem_in, sem_k, sem_v, s_d, r_d, s_rs, r_rs, s_ag, r_ag, s_e, r_e):
    tp = lax.axis_index("tp")
    core = tp % 2
    chip = tp // 2
    nch = B // CH
    first = R0 // CH
    ngr = (B - R0) // NG
    HR = CH // 2
    QC = D // 4

    def kcopy(i, a, b, sem):
        return pltpu.make_async_copy(a.at[pl.ds(R0 + NG * i, NG)], b.at[pl.ds(NG * i, NG)], sem.at[i])

    per = CH // NG
    for c in range(nch - first):
        for i in range(per):
            kcopy(c * per + i, k_h, k2, sem_k).start()
        for i in range(per):
            kcopy(c * per + i, v_h, v2, sem_v).start()
        if c == 0:
            c_wo = pltpu.make_async_copy(wo_h, wo_v, sem_in.at[0])
            c_wo.start()
            c_x = pltpu.make_async_copy(x_h, x_v, sem_in.at[1])
            c_x.start()

    sib = tp + 1 - 2 * core
    peers = []
    for k in range(1, 4):
        chip_k = (chip // 2 + k // 2) % 2 * 2 + (chip % 2 + k % 2) % 2
        peers.append((chip_k, chip_k * 2 + core))

    barrier = pltpu.get_barrier_semaphore()
    for t in [sib] + [p for _, p in peers]:
        pl.semaphore_signal(barrier, inc=1, device_id={"tp": t}, device_id_type=MESH)
    pl.semaphore_wait(barrier, 4)

    def part_of(c):
        return part_i.at[pl.ds(c * CH, CH)] if c < first else part_v.at[pl.ds((c - first) * CH, CH)]

    my_rows = pl.ds(pl.multiple_of(core * HR, HR), HR)
    sib_rows = pl.ds(pl.multiple_of((1 - core) * HR, HR), HR)
    my_cols = pl.ds(pl.multiple_of(chip * QC, QC), QC)

    def remote(src, dst, s, r, t):
        return pltpu.make_async_remote_copy(src_ref=src, dst_ref=dst, send_sem=s, recv_sem=r, device_id={"tp": t}, device_id_type=MESH)

    def a_copy(c):
        return remote(part_of(c).at[sib_rows], d2_v.at[c], s_d.at[c], r_d.at[c], sib)

    def b_copies(c):
        return [remote(sum_v.at[c, :, pl.ds(pl.multiple_of(ck * QC, QC), QC)], rs_v.at[c, k], s_rs.at[c, k], r_rs.at[c, k], t)
                for k, (ck, t) in enumerate(peers)]

    def out_rows(c):
        return pl.ds(pl.multiple_of(c * CH + core * HR, HR), HR)

    def c_copies(c):
        piece = gat_v.at[out_rows(c), my_cols]
        return [remote(piece, piece, s_ag.at[c, k], r_ag.at[c, k], t) for k, (_, t) in enumerate(peers)]

    def d_copy(c):
        rows = gat_v.at[out_rows(c)]
        return remote(rows, rows, s_e.at[c], r_e.at[c], sib)

    def step_a(c):
        a_copy(c).start()

    def step_b(c):
        a_copy(c).wait_recv()
        own = part_of(c)
        sum_v[c] = (own[my_rows, :].astype(F32) + d2_v[c].astype(F32)).astype(BF16)
        for cp in b_copies(c):
            cp.start()

    def step_c(c):
        tot = sum_v[c, :, my_cols].astype(F32)
        for k, cp in enumerate(b_copies(c)):
            cp.wait_recv()
            tot = tot + rs_v[c, k].astype(F32)
        tot = tot + x_v[out_rows(c), my_cols].astype(F32)
        gat_v[out_rows(c), my_cols] = tot.astype(BF16)
        for cp in c_copies(c):
            cp.start()

    def step_d(c):
        for cp in c_copies(c):
            cp.wait_recv()
        d_copy(c).start()

    def attend_scores(c):
        build_queries(q_i, c * CH, qt_v)
        acc = jnp.zeros((S, 2 * CH), F32)

        def score_step(j, acc):
            i = (c - first) * per + j
            kcopy(i, k_h, k2, sem_k).wait()
            return scores_of_group(pos_s, kn_i, k2, qt_v, acc, R0 + i * NG, i * NG, j * NG)

        acc = lax.fori_loop(0, per, score_step, acc)
        p_v[...] = softmax_slots(acc, pos_i, c)

    def attend_context(c):
        @pl.loop(0, per)
        def _(j):
            i = (c - first) * per + j
            kcopy(i, v_h, v2, sem_v).wait()
            context_of_group(pos_s, vn_i, v2, p_v, ctx_v, R0 + i * NG, i * NG, j * NG)

        if c == first:
            c_wo.wait()
            c_x.wait()
        for n in range(8):
            cs = pl.ds(256 * n, 256)
            part_v[pl.ds((c - first) * CH, CH), cs] = (dot(ctx_v[...], wo_v[:, cs]) + m_i[pl.ds(c * CH, CH), cs]).astype(BF16)

    step_a(0)
    attend_scores(1)
    step_b(0)
    attend_context(1)
    step_a(1)
    attend_scores(2)
    step_b(1)
    attend_context(2)
    step_a(2)
    step_c(0)
    attend_scores(3)
    step_b(2)
    attend_context(3)
    step_a(3)
    step_c(1)
    step_d(0)
    step_b(3)
    step_c(2)
    step_d(1)
    step_c(3)
    step_d(2)
    step_d(3)
    for c in range(nch):
        a_copy(c).wait_send()
        for cp in b_copies(c):
            cp.wait_send()
        for cp in c_copies(c):
            cp.wait_send()
        d_copy(c).wait()
    out_o[...] = gat_v[...]


def write_kernel(k_i, v_i, o_i, k0_h, v0_h, ko_h, vo_h, o_h, sem):
    n = (B - R0) // NG // 2
    copies = []
    for i in range(n):
        rows = pl.ds(2 * NG * i, 2 * NG)
        dst = pl.ds(R0 + 2 * NG * i, 2 * NG)
        copies.append(pltpu.make_async_copy(k_i.at[rows], ko_h.at[dst], sem.at[2 * i]))
        copies.append(pltpu.make_async_copy(v_i.at[rows], vo_h.at[dst], sem.at[2 * i + 1]))
    copies.append(pltpu.make_async_copy(o_i, o_h, sem.at[2 * n]))
    for c in copies:
        c.start()
    for c in copies:
        c.wait()


def solution(mesh):
    row_spec = P('dp', None)
    vec_spec = P(None)
    cache_spec = P('dp', 'tp', None, None)
    vm = pl.BlockSpec(memory_space=pltpu.VMEM)
    sm = pl.BlockSpec(memory_space=pltpu.SMEM)
    anyspace = pl.BlockSpec(memory_space=pl.ANY)
    dma = pltpu.SemaphoreType.DMA
    MIB = 1024 * 1024

    def hbm(t):
        return pltpu.with_memory_space_constraint(t, pltpu.HBM)

    def device_step(x, ln_attn_gamma, ln_attn_beta, ln_mlp_gamma, ln_mlp_beta, w_qkv, w_out, w_up, w_down, k_cache, v_cache, positions):
        wq = w_qkv.transpose(0, 2, 1, 3).reshape(D * 3 * G, H)
        wo = w_out.reshape(G * H, D)
        pos2 = positions.reshape(2, 128)
        cache = jax.ShapeDtypeStruct((B, G, S, H), BF16)
        NR = B - R0
        k0, v0, q, kn, vn, m, part = pl.pallas_call(
            local_kernel,
            out_shape=(cache, cache) + (pltpu.VMEM((B, G * H), F32),) * 3 + (pltpu.VMEM((B, D), F32), pltpu.VMEM((R0, D), BF16)),
            in_specs=[anyspace] * 11 + [sm, anyspace],
            out_specs=(anyspace, anyspace) + (vm,) * 5,
            scratch_shapes=[
                pltpu.VMEM((B, D), BF16), pltpu.VMEM((32, D), F32), pltpu.VMEM((D * 3 * G, H), BF16), pltpu.VMEM((768, H), F32),
                pltpu.VMEM((D, 768), BF16), pltpu.VMEM((G * H, D), BF16), pltpu.VMEM((D, FL), BF16), pltpu.VMEM((FL, D), BF16),
                pltpu.VMEM((R0, G, S, H), BF16), pltpu.VMEM((R0, G, S, H), BF16), pltpu.VMEM((2, 128), jnp.int32),
                pltpu.VMEM((B, D), BF16), pltpu.VMEM((B, D), BF16), pltpu.VMEM((B, H), F32), pltpu.VMEM((B, H), F32),
                pltpu.VMEM((B, FL), BF16), pltpu.VMEM((G * H, 2 * CH), BF16), pltpu.VMEM((2 * CH, S), BF16), pltpu.VMEM((CH, G * H), BF16),
                pltpu.VMEM((R0, D), F32),
                dma((15,)), dma((R0 // NG,)), dma((R0 // NG,)), dma((R0 // NG,)), dma((R0 // NG,)),
            ],
            compiler_params=pltpu.CompilerParams(vmem_limit_bytes=40 * MIB),
            name="local_part",
        )(hbm(x), *[hbm(t.reshape(1, D)) for t in (ln_attn_gamma, ln_attn_beta, ln_mlp_gamma, ln_mlp_beta)],
          hbm(wq), hbm(wo), hbm(w_up), hbm(w_down), hbm(k_cache), hbm(v_cache), positions, hbm(pos2))

        nch = B // CH
        k2, v2, o = pl.pallas_call(
            reduce_kernel,
            out_shape=(pltpu.VMEM((NR, G, S, H), BF16), pltpu.VMEM((NR, G, S, H), BF16), pltpu.VMEM((B, D), BF16)),
            in_specs=[anyspace] * 4 + [vm] * 5 + [sm, vm],
            out_specs=(vm,) * 3,
            scratch_shapes=[
                pltpu.VMEM((B, D), BF16), pltpu.VMEM((G * H, D), BF16), pltpu.VMEM((G * H, 2 * CH), BF16), pltpu.VMEM((2 * CH, S), BF16),
                pltpu.VMEM((CH, G * H), BF16), pltpu.VMEM((NR, D), BF16), pltpu.VMEM((nch, CH // 2, D), BF16),
                pltpu.VMEM((nch, CH // 2, D), BF16), pltpu.VMEM((nch, 3, CH // 2, D // 4), BF16), pltpu.VMEM((B, D), BF16),
                dma((2,)), dma((NR // NG,)), dma((NR // NG,)),
                dma((nch,)), dma((nch,)), dma((nch, 3)), dma((nch, 3)), dma((nch, 3)), dma((nch, 3)), dma((nch,)), dma((nch,)),
            ],
            compiler_params=pltpu.CompilerParams(vmem_limit_bytes=16 * MIB, collective_id=0, has_side_effects=True),
            name="reduce_part",
        )(hbm(x), hbm(wo), hbm(k_cache), hbm(v_cache), q, kn, vn, m, part, positions, pos2)

        kf, vf, out = pl.pallas_call(
            write_kernel,
            out_shape=(cache, cache, jax.ShapeDtypeStruct((B, D), BF16)),
            in_specs=[vm] * 3 + [anyspace] * 2,
            out_specs=(anyspace,) * 3,
            scratch_shapes=[dma((NR // NG + 1,))],
            input_output_aliases={3: 0, 4: 1},
            compiler_params=pltpu.CompilerParams(vmem_limit_bytes=4 * MIB),
            name="write_part",
        )(k2, v2, o, k0, v0)
        return out, kf, vf

    return jax.shard_map(device_step, mesh=mesh, in_specs=(row_spec, vec_spec, vec_spec, vec_spec, vec_spec, P(None, 'tp', None, None), P('tp', None, None, None), P(None, 'tp'), P('tp', None), cache_spec, cache_spec, P('dp')), out_specs=(row_spec, cache_spec, cache_spec), check_vma=False)
```

time: 142 us -> 51.4 us (0.36)
  waiting for transfers between devices: 53.1 us -> 0 us
  Pallas kernels: 0 us -> 50.6 us
  matrix products: 33.8 us -> 0 us
  other arithmetic: 31.5 us -> 0 us
  between operations: 14.2 us -> 0.67 us
  local copies, waits for them, and re-layouts: 9.15 us -> 0.01 us
    psum x1 -> x0, waiting for transfers between devices: 53.1 us -> none  [device_step(): mlp_total = lax.psum(mlp_part, 'tp')]
    pallas_call x0 -> x3, Pallas kernels: none -> 50.6 us  [the longest x1 29.3 us: device_step(): pl.pallas_call(reduce_kernel, out_shape=(pltpu.VMEM((NR, G, S, H), BF16),...]
    dot_general x4 -> x0, matrix products: 30.7 us -> none  [the longest x1 12.2 us: attend_local(): jnp.einsum('bgqh,bgsh->bgqs', queries, keys_all, preferred_element_type=j...]
    select_n x1 -> x0, other arithmetic: 23 us -> none  [attend_local(): keys_all = jnp.where(write_mask, new_key[:, :, None, :], k_cache)]
    unnamed x13 -> x2, local copies, waits for them, and re-layouts: 8.76 us -> 0.01 us
    convert_element_type x4 -> x0, other arithmetic: 3.92 us -> none  [the longest x1 3.05 us: device_step(): (x.astype(jnp.float32) + attn_total.astype(jnp.float32) + mlp_total.astyp...]
    reduce_sum x2 -> x0, other arithmetic: 3.09 us -> none  [the longest x1 1.64 us: layer_norm(): row_var = jnp.mean(centred * centred, axis=-1, keepdims=True)]
    unnamed x1 -> x0, matrix products: 3.04 us -> none
  transfers between devices with their start and end apart: 1 -> 0, of which waited for: 1 -> 0; matrix products, arithmetic and copies ran while one was open for 0% -> 0% of each run, Pallas kernels for 0% -> 0%
where the time goes in v1:
time: 51.4 us; the launch traced here: 51.3 us
  Pallas kernels  50.6 us (98%)
  between operations  0.67 us (1%)
    pallas_call x1, Pallas kernels, device_step(): pl.pallas_call(reduce_kernel, out_shape=(pltpu.VMEM((NR, G, S, H), BF16),...  29.3 us
    pallas_call x1, Pallas kernels, device_step(): pl.pallas_call(local_kernel, out_shape=(cache, cache) + (pltpu.VMEM((B, G...  12.5 us
    pallas_call x1, Pallas kernels, device_step(): pl.pallas_call(write_kernel, out_shape=(cache, cache, jax.ShapeDtypeStruc...  8.78 us

profile of v1, /device:TPU:0, one launch (start us, length us, event | category | flops | bytes accessed | tf_op | source)
XLA Modules:
  0.0 51.3 jit_solution(640023599199648010)
XLA Ops:
  0.6 0.0 copy-start
  0.6 12.5 %local_part.1 = (bf16[256,2,128,128]{3,2,1,0:T(8,128)(2,1)}, bf16[256,2,128,128]{3,2,1,0:T(8,128)(2,1)}, f32[256,256]{1,0:T(8,128)S(1)}, f32[256,256]{1,0:T(8,12...) custom-call(bf16[256,2048]{1,0:T(8,128)(2,1)} %x_h.3, f32[1,2048]{1,0:T(1,128)} %bitcast.14, ...), custom_call_target="tpu_custom_call" | custom-call | tf_op jit(solution)/shard_map/local_part/pallas_call | solution.py:425
  13.2 0.0 copy-done
  13.2 29.3 %reduce_part.1 = (bf16[192,2,128,128]{3,2,1,0:T(8,128)(2,1)S(1)}, bf16[192,2,128,128]{3,2,1,0:T(8,128)(2,1)S(1)}, bf16[256,2048]{1,0:T(8,128)(2,1)S(1)}) custom-call(bf16[256,2048]{1,0:T(8,128)(2,1)} %x_h.3, bf16[256,2048]{1,0:T(8,128)(2,1)} %bitcast.12, bf16[256,2,128,128]{3,2,1,0:T(8,128)(2,1)} %k_h.3, bf16[256,2,128,128]{3,2,1,0:T(8,128)(2,1)} %v_h.3, ...), custom_call_target="tpu_custom_call" | custom-call | tf_op jit(solution)/shard_map/reduce_part/pallas_call | solution.py:445
  42.5 8.8 %write_part.1 = (bf16[256,2,128,128]{3,2,1,0:T(8,128)(2,1)}, bf16[256,2,128,128]{3,2,1,0:T(8,128)(2,1)}, bf16[256,2048]{1,0:T(8,128)(2,1)}) custom-call(bf16[192,2,128,128]{3,2,1,0:T(8,128)(2,1)S(1)} %get-tuple-element.21.k_i, bf16[192,2,128,128]{3,2,1,0:T(8,128)(2,1)S(1)} %get-tuple-element.22.v_i, ...), custom_call_target="tpu_custom_call", output_to_operand_aliasing={{0}: (3, {}), {1}: (4, {})} | custom-call | tf_op jit(solution)/shard_map/write_part/pallas_call | solution.py:461
Async XLA Ops:
  0.6 12.5 %copy-start = (s32[256]{0:T(256)S(1)}, s32[256]{0:T(256)}, u32[]{:S(2)}) copy-start(s32[256]{0:T(256)} %pos_s.3) | copy-start | bytes 3076

commit v2 on v1

v2 whole, which is shorter than its diff:
```python
import functools
import math

import jax
import jax.numpy as jnp
from jax import lax
from jax.experimental import pallas as pl
from jax.experimental.pallas import tpu as pltpu
from jax.sharding import PartitionSpec as P

LN_EPS = 1e-5
ROPE_BASE = 10000.0
NEG_BIG = -1e30
MESH = pl.DeviceIdType.MESH
F32 = jnp.float32
BF16 = jnp.bfloat16

B = 256
D = 2048
S = 128
H = 128
G = 2
FL = 1024
R0 = 64
CH = 64
NG = 16
GI = 2
SCALE = H ** -0.5
PER = CH // NG


def dot(a, b):
    return jnp.dot(a, b, preferred_element_type=F32)


def iota(shape, dim):
    return lax.broadcasted_iota(jnp.int32, shape, dim)


def build_queries(q_ref, row, qt_ref):
    stacked = jnp.concatenate([q_ref[pl.ds(row, CH), pl.ds(0, H)], q_ref[pl.ds(row, CH), pl.ds(H, H)]], axis=0)
    turned = stacked.T
    low = iota((H, 2 * CH), 1) < CH
    qt_ref[pl.ds(0, H), :] = jnp.where(low, turned, 0.0).astype(BF16)
    qt_ref[pl.ds(H, H), :] = jnp.where(low, 0.0, turned).astype(BF16)


def add_rows(buf, new_ref, pos_s, row, at):
    rows = pl.ds(row if isinstance(row, int) else pl.multiple_of(row, NG), NG)
    new = [new_ref[rows, pl.ds(g * H, H)] for g in range(G)]
    inside = iota((NG, H), 0).astype(F32).astype(BF16)
    for u in range(NG):
        pos = pos_s[row + u]
        start = pl.multiple_of(lax.shift_left(lax.shift_right_logical(pos, 4), 4), NG)
        mask = inside == jnp.full((NG, H), (pos - start).astype(F32), F32).astype(BF16)
        for g in range(G):
            tile = buf.at[at + u, g, pl.ds(start, NG), :]
            tile[...] = jnp.where(mask, jnp.broadcast_to(new[g][u:u + 1], (NG, H)).astype(BF16), tile[...])


def scores_of_group(kbuf, qt_ref, acc, at, local):
    lane = iota((S, 2 * CH), 1) & (CH - 1)
    for u in range(NG):
        keys = jnp.concatenate([kbuf[at + u, g] for g in range(G)], axis=1)
        acc = jnp.where(lane == local + u, dot(keys, qt_ref[...]), acc)
    return acc


def attend_scores(c, at, wait, also, kbuf, q_ref, kn_ref, pos_v, qt_v, p_v, pn_v):
    build_queries(q_ref, c * CH, qt_v)
    rows = pl.ds(c * CH, CH)
    with_new = jnp.concatenate([q_ref[rows, pl.ds(g * H, H)] * kn_ref[rows, pl.ds(g * H, H)] for g in range(G)], axis=0)
    s_new = jnp.sum(with_new.T, axis=0, keepdims=True)
    new_at = pos_columns(pos_v, c)

    def step(j, acc):
        for w in range(GI):
            wait(j * GI + w)
        for w in range(GI):
            i = j * GI + w
            acc = scores_of_group(kbuf, qt_v, acc, at + i * NG, i * NG)
            also(i)
        return acc

    acc = lax.fori_loop(0, CH // NG // GI, step, jnp.zeros((S, 2 * CH), F32))
    slot = iota((S, 2 * CH), 0)
    s = jnp.where(slot < new_at, acc * SCALE, jnp.where(slot == new_at, s_new * SCALE, NEG_BIG))
    p = softmax_slots(s).astype(BF16).astype(F32)
    p_v[...] = jnp.where(slot == new_at, 0.0, p).T.astype(BF16)
    p_new = jnp.sum(jnp.where(slot == new_at, p, 0.0), axis=0, keepdims=True)
    pn_v[...] = jnp.broadcast_to(p_new, (2 * CH, H)).T


def attend_context(c, at, lo, hi, wait, also, vbuf, vn_ref, p_v, pn_v, ctx_v):
    @pl.loop(0, (hi - lo) // GI)
    def _(j):
        for w in range(GI):
            wait(lo + j * GI + w)
        for w in range(GI):
            i = lo + j * GI + w
            ctx = context_of_group(vbuf, p_v, at + i * NG, i * NG)
            rows = pl.ds(pl.multiple_of(c * CH + i * NG, NG), NG)
            for g in range(G):
                new = pn_v[pl.ds(pl.multiple_of(g * CH + i * NG, NG), NG), :] * vn_ref[rows, pl.ds(g * H, H)]
                ctx_v[pl.ds(pl.multiple_of(i * NG, NG), NG), pl.ds(g * H, H)] = (ctx[g] + new).astype(BF16)
            also(i)


def pos_columns(pos_v, chunk):
    row = pos_v[pl.ds(chunk // 2, 1), :]
    lane = iota((1, 2 * CH), 1)
    turned = pltpu.roll(row, CH, 1)
    return jnp.where(lane < CH, row, turned) if chunk % 2 == 0 else jnp.where(lane < CH, turned, row)


def softmax_slots(s):
    e = jnp.exp(s - jnp.max(s, axis=0, keepdims=True))
    return e / jnp.sum(e, axis=0, keepdims=True)


def context_of_group(vbuf, p_ref, at, local):
    rows16 = iota((NG, S), 0).astype(F32).astype(BF16)
    zero = jnp.zeros((NG, S), BF16)
    total = []
    for g in range(G):
        probs = p_ref[pl.ds(pl.multiple_of(g * CH + local, NG), NG), :]
        tot = None
        for u in range(0, NG, 2):
            ps = [jnp.where(rows16 == jnp.asarray(u + w, BF16), probs, zero) for w in range(2)]
            vs = [vbuf[at + u + w, g] for w in range(2)]
            part = dot(jnp.concatenate(ps, axis=1), jnp.concatenate(vs, axis=0))
            tot = part if tot is None else tot + part
        total.append(tot)
    return total


def local_kernel(x_h, ga_h, ba_h, gm_h, bm_h, wq_h, wo_h, wu_h, wd_h, k_h, v_h, pos_s, pos_h,
                 ko_h, vo_h, q_o, kn_o, vn_o, m_o, part_o, x_v, wo_v, kp_o,
                 ln_v, wq_v, w32_v, wqb_v, wu_v, wd_v, kb, vb, pos_v, ain_v, min_v, cos_v, sin_v, h_v, qt_v, p_v, pn_v, ctx_v, a_v,
                 sem_in, sem_k, sem_v, sem_ko, sem_vo, sem_kp):
    ngr = R0 // NG

    def rd(src, dst, i):
        c = pltpu.make_async_copy(src, dst, sem_in.at[i])
        c.start()
        return c

    c_pos = rd(pos_h, pos_v, 0)
    c_x = [rd(x_h.at[pl.ds(64 * i, 64)], x_v.at[pl.ds(64 * i, 64)], 15 + i) for i in range(4)]
    c_ln = [rd(r, ln_v.at[pl.ds(8 * i, 1)], 2 + i) for i, r in enumerate((ga_h, ba_h, gm_h, bm_h))]
    c_wq = [rd(wq_h.at[pl.ds(3072 * i, 3072)], wq_v.at[pl.ds(3072 * i, 3072)], 6 + i) for i in range(4)]

    def kcopy(i, a, b, sem):
        return pltpu.make_async_copy(a.at[pl.ds(NG * i, NG)], b.at[pl.ds(NG * i, NG)], sem.at[i])

    kp_copies = [pltpu.make_async_copy(k_h.at[pl.ds(R0 + NG * i, NG)], kp_o.at[pl.ds(NG * i, NG)], sem_kp.at[i]) for i in range(PER)]

    c_pos.wait()
    lane = iota((S, H), 1)
    inv = jnp.exp((lane & (H // 2 - 1)).astype(F32) * (-2.0 * math.log(ROPE_BASE) / H))
    for i in range(2):
        at = jnp.broadcast_to(pos_v[pl.ds(i, 1), :].astype(F32), (S, H)).T
        ang = at * inv
        sn = jnp.sin(ang)
        cos_v[pl.ds(S * i, S), :] = jnp.cos(ang)
        sin_v[pl.ds(S * i, S), :] = jnp.where(lane < H // 2, -sn, sn)

    for c in c_ln + c_x:
        c.wait()
    for i in range(PER):
        kcopy(i, k_h, kb, sem_k).start()
    RB = 16
    NB = 4

    @pl.loop(0, B // (RB * NB))
    def _(i):
        rows = [pl.ds(pl.multiple_of(i * (RB * NB) + RB * w, RB), RB) for w in range(NB)]

        def tile(r, j):
            return x_v[r, pl.ds(128 * j, 128)].astype(F32)

        means, scales = [], []
        for r in rows:
            tot = tile(r, 0)
            for j in range(1, 16):
                tot = tot + tile(r, j)
            means.append(jnp.sum(tot, axis=-1, keepdims=True) * (1.0 / D))
        for r, mean in zip(rows, means):
            tot = jnp.zeros((RB, 128), F32)
            for j in range(16):
                d = tile(r, j) - mean
                tot = tot + d * d
            scales.append(lax.rsqrt(jnp.sum(tot, axis=-1, keepdims=True) * (1.0 / D) + LN_EPS))
        for r, mean, rs in zip(rows, means, scales):
            for j in range(16):
                cs = pl.ds(128 * j, 128)
                n = (tile(r, j) - mean) * rs
                ain_v[r, cs] = (n * ln_v[pl.ds(0, 1), cs] + ln_v[pl.ds(8, 1), cs]).astype(BF16)
                min_v[r, cs] = (n * ln_v[pl.ds(16, 1), cs] + ln_v[pl.ds(24, 1), cs]).astype(BF16)

    for c in c_wq:
        c.wait()
    for i in range(PER):
        kcopy(i, v_h, vb, sem_v).start()
    c_wo = rd(wo_h, wo_v, 10)
    c_wu = [rd(wu_h.at[pl.ds(1024 * i, 1024)], wu_v.at[pl.ds(1024 * i, 1024)], 11 + i) for i in range(2)]

    @pl.loop(0, 16)
    def _(i):
        w32_v[...] = wq_v[pl.ds(pl.multiple_of(i * 768, 768), 768), :].astype(F32)
        for j in range(3):
            for g in range(G):
                wqb_v[pl.ds(pl.multiple_of(i * 128, 128), 128), pl.ds((g * 3 + j) * H, H)] = (
                    w32_v[pl.ds(2 * j + g, 128, stride=6), :].astype(BF16))

    def rotary(u, r):
        return u * cos_v[r, :] + pltpu.roll(u, H // 2, 1) * sin_v[r, :]

    for n in range(3):
        qkv = dot(ain_v[...], wqb_v[:, pl.ds(256 * n, 256)]).astype(BF16).astype(F32)
        for w in range(2):
            g, j = divmod(2 * n + w, 3)
            u = qkv[:, w * H:(w + 1) * H]
            dst = (q_o, kn_o, vn_o)[j]
            if j < 2:
                u = rotary(u, pl.ds(0, B)).astype(BF16).astype(F32)
            dst[:, pl.ds(g * H, H)] = u

    for c in range(R0 // CH):
        c_wd = [rd(wd_h.at[pl.ds(512 * i, 512)], wd_v.at[pl.ds(512 * i, 512)], 13 + i) for i in range(2)]
        base = c * CH

        def wait_k(i, c=c):
            kcopy(c * PER + i, k_h, kb, sem_k).wait()

        def wait_v(i, c=c):
            kcopy(c * PER + i, v_h, vb, sem_v).wait()

        def old_v(i, c=c):
            if c > 0:
                add_rows(vb, vn_o, pos_s, base - CH + i * NG, base - CH + i * NG)

        def add_k(i):
            add_rows(kb, kn_o, pos_s, base + i * NG, base + i * NG)

        attend_scores(c, base, wait_k, old_v, kb, q_o, kn_o, pos_v, qt_v, p_v, pn_v)
        if c > 0:
            for j in range(PER):
                kcopy((c - 1) * PER + j, vb, vo_h, sem_vo).start()
        for cp in kp_copies:
            cp.start()
        attend_context(c, base, 0, PER, wait_v, add_k, vb, vn_o, p_v, pn_v, ctx_v)
        if c == 0:
            c_wo.wait()
        for n in range(8):
            a_v[pl.ds(base, CH), pl.ds(256 * n, 256)] = dot(ctx_v[...], wo_v[:, pl.ds(256 * n, 256)])
        for j in range(PER):
            kcopy(c * PER + j, kb, ko_h, sem_ko).start()

    for c in c_wu:
        c.wait()
    for n in range(4):
        u = dot(min_v[...], wu_v[:, pl.ds(256 * n, 256)])
        h_v[:, pl.ds(256 * n, 256)] = (0.5 * u * (1.0 + lax.erf(u * (2.0 ** -0.5)))).astype(BF16)
        add_rows(vb, vn_o, pos_s, R0 - CH + n * NG, R0 - CH + n * NG)
    for j in range(PER):
        kcopy(R0 // NG - PER + j, vb, vo_h, sem_vo).start()
    for c in c_wd:
        c.wait()
    for n in range(8):
        cs = pl.ds(256 * n, 256)
        m_o[:, cs] = dot(h_v[...], wd_v[:, cs])
        part_o[:, cs] = (a_v[:, cs] + m_o[pl.ds(0, R0), cs]).astype(BF16)

    for cp in kp_copies:
        cp.wait()
    for i in range(ngr):
        kcopy(i, kb, ko_h, sem_ko).wait()
        kcopy(i, vb, vo_h, sem_vo).wait()


PARTS = ((0, 64), (64, 64), (128, 64), (192, 32), (224, 32))


def reduce_kernel(k_h, v_h, q_i, kn_i, vn_i, m_i, part_i, x_v, wo_v, kp_i, pos_i,
                  k2, v2, out_o,
                  qt_v, p_v, pn_v, ctx_v, part_v, d2_v, sum_v, rs_v, gat_v,
                  sem_k, sem_v, s_d, r_d, s_rs, r_rs, s_ag, r_ag, s_e, r_e):
    tp = lax.axis_index("tp")
    core = tp % 2
    chip = tp // 2
    first = R0 // CH
    per = CH // NG
    QC = D // 4

    def kcopy(i):
        return pltpu.make_async_copy(k_h.at[pl.ds(R0 + CH + NG * i, NG)], k2.at[pl.ds(NG * i, NG)], sem_k.at[i])

    def vcopy(i):
        return pltpu.make_async_copy(v_h.at[pl.ds(R0 + NG * i, NG)], v2.at[pl.ds(NG * i, NG)], sem_v.at[i])

    def issue_k(c):
        for i in range(per):
            kcopy((c - first - 1) * per + i).start()

    def issue_v(c):
        for i in range(per):
            vcopy((c - first) * per + i).start()

    issue_v(1)
    issue_k(2)

    sib = tp + 1 - 2 * core
    peers = []
    for k in range(1, 4):
        chip_k = (chip // 2 + k // 2) % 2 * 2 + (chip % 2 + k % 2) % 2
        peers.append((chip_k, chip_k * 2 + core))

    barrier = pltpu.get_barrier_semaphore()
    for t in [sib] + [p for _, p in peers]:
        pl.semaphore_signal(barrier, inc=1, device_id={"tp": t}, device_id_type=MESH)
    my_cols = pl.ds(pl.multiple_of(chip * QC, QC), QC)

    def remote(src, dst, s, r, t):
        return pltpu.make_async_remote_copy(src_ref=src, dst_ref=dst, send_sem=s, recv_sem=r, device_id={"tp": t}, device_id_type=MESH)

    def part_of(c, which):
        start, n = PARTS[c]
        ref, base = (part_i, start) if start < R0 else (part_v, start - R0)
        return ref.at[pl.ds(pl.multiple_of(base + which * (n // 2), NG), n // 2)]

    def half(c):
        start, n = PARTS[c]
        return pl.ds(start // 2, n // 2)

    def out_rows(c):
        start, n = PARTS[c]
        return pl.ds(pl.multiple_of(start + core * (n // 2), NG), n // 2)

    def a_copy(c):
        return remote(part_of(c, 1 - core), d2_v.at[half(c)], s_d.at[c], r_d.at[c], sib)

    def b_copies(c):
        return [remote(sum_v.at[half(c), pl.ds(pl.multiple_of(ck * QC, QC), QC)], rs_v.at[k, half(c)], s_rs.at[c, k], r_rs.at[c, k], t)
                for k, (ck, t) in enumerate(peers)]

    def c_copies(c):
        piece = gat_v.at[out_rows(c), my_cols]
        return [remote(piece, piece, s_ag.at[c, k], r_ag.at[c, k], t) for k, (_, t) in enumerate(peers)]

    def d_copy(c):
        rows = gat_v.at[out_rows(c)]
        return remote(rows, rows, s_e.at[c], r_e.at[c], sib)

    def step_a(c):
        a_copy(c).start()

    def step_b(c):
        a_copy(c).wait_recv()
        sum_v[half(c)] = (part_of(c, core)[...].astype(F32) + d2_v[half(c)].astype(F32)).astype(BF16)
        for cp in b_copies(c):
            cp.start()

    def step_c(c):
        tot = sum_v[half(c), my_cols].astype(F32) + x_v[out_rows(c), my_cols].astype(F32)
        for k, cp in enumerate(b_copies(c)):
            cp.wait_recv()
            tot = tot + rs_v[k, half(c)].astype(F32)
        gat_v[out_rows(c), my_cols] = tot.astype(BF16)
        for cp in c_copies(c):
            cp.start()

    def step_d(c):
        for cp in c_copies(c):
            cp.wait_recv()
        d_copy(c).start()

    def nothing(i):
        pass

    def scores(c):
        if c == first:
            attend_scores(c, 0, nothing, nothing, kp_i, q_i, kn_i, pos_i, qt_v, p_v, pn_v)
        else:
            at = (c - first - 1) * per
            attend_scores(c, at * NG, lambda i: kcopy(at + i).wait(), nothing, k2, q_i, kn_i, pos_i, qt_v, p_v, pn_v)

    def context(c, lo, hi):
        at = (c - first) * CH
        attend_context(c, at, lo, hi, lambda i: vcopy((c - first) * per + i).wait(), nothing, v2, vn_i, p_v, pn_v, ctx_v)
        n = (hi - lo) * NG
        for k in range(8):
            cs = pl.ds(256 * k, 256)
            part_v[pl.ds(at + lo * NG, n), cs] = (
                dot(ctx_v[pl.ds(lo * NG, n), :], wo_v[:, cs]) + m_i[pl.ds(c * CH + lo * NG, n), cs]).astype(BF16)

    pl.semaphore_wait(barrier, 4)
    step_a(0)
    scores(1)
    step_b(0)
    issue_v(2)
    context(1, 0, per)
    step_a(1)
    issue_k(3)
    scores(2)
    step_b(1)
    step_c(0)
    issue_v(3)
    context(2, 0, per)
    step_a(2)
    scores(3)
    step_b(2)
    context(3, 0, per // 2)
    step_a(3)
    step_c(1)
    context(3, per // 2, per)
    step_a(4)
    step_b(3)
    step_b(4)
    step_d(0)
    step_c(2)
    step_d(1)
    step_c(3)
    step_c(4)
    step_d(2)
    step_d(3)
    step_d(4)
    for c in range(len(PARTS)):
        a_copy(c).wait_send()
        for cp in b_copies(c):
            cp.wait_send()
        for cp in c_copies(c):
            cp.wait_send()
        d_copy(c).wait()
    out_o[...] = gat_v[...]


def write_kernel(kp_i, k_i, v_i, o_i, kn_i, vn_i, pos_s, k0_h, v0_h, kp3, k3, v3, ko_h, vo_h, o_h, sem):
    n = (B - R0) // NG
    c_out = pltpu.make_async_copy(o_i, o_h, sem.at[2 * n])
    c_out.start()

    def copy(src, dst, i, k):
        return pltpu.make_async_copy(src.at[pl.ds(NG * i, NG)], dst.at[pl.ds(R0 + NG * k, NG)], sem.at[k if dst is ko_h else n + k])

    for src, dst, new, first, count in ((kp3, ko_h, kn_i, 0, PER), (v3, vo_h, vn_i, 0, n), (k3, ko_h, kn_i, PER, n - PER)):
        @pl.loop(0, count)
        def _(i, src=src, dst=dst, new=new, first=first):
            add_rows(src, new, pos_s, R0 + (first + i) * NG, i * NG)

            @pl.when(i > 0)
            def _():
                copy(src, dst, i - 1, first + i - 1).start()

        copy(src, dst, count - 1, first + count - 1).start()

    for src, dst, first, count in ((kp3, ko_h, 0, PER), (v3, vo_h, 0, n), (k3, ko_h, PER, n - PER)):
        @pl.loop(0, count)
        def _(i, src=src, dst=dst, first=first):
            copy(src, dst, i, first + i).wait()

    c_out.wait()


def solution(mesh):
    row_spec = P('dp', None)
    vec_spec = P(None)
    cache_spec = P('dp', 'tp', None, None)
    vm = pl.BlockSpec(memory_space=pltpu.VMEM)
    sm = pl.BlockSpec(memory_space=pltpu.SMEM)
    anyspace = pl.BlockSpec(memory_space=pl.ANY)
    dma = pltpu.SemaphoreType.DMA
    MIB = 1024 * 1024

    def hbm(t):
        return pltpu.with_memory_space_constraint(t, pltpu.HBM)

    def device_step(x, ln_attn_gamma, ln_attn_beta, ln_mlp_gamma, ln_mlp_beta, w_qkv, w_out, w_up, w_down, k_cache, v_cache, positions):
        wq = w_qkv.transpose(0, 2, 1, 3).reshape(D * 3 * G, H)
        wo = w_out.reshape(G * H, D)
        pos2 = positions.reshape(2, 128)
        cache = jax.ShapeDtypeStruct((B, G, S, H), BF16)
        NR = B - R0
        k0, v0, q, kn, vn, m, part, xv, wov, kp = pl.pallas_call(
            local_kernel,
            out_shape=(cache, cache) + (pltpu.VMEM((B, G * H), F32),) * 3 + (pltpu.VMEM((B, D), F32), pltpu.VMEM((R0, D), BF16), pltpu.VMEM((B, D), BF16),
                                                                              pltpu.VMEM((G * H, D), BF16), pltpu.VMEM((CH, G, S, H), BF16)),
            in_specs=[anyspace] * 11 + [sm, anyspace],
            out_specs=(anyspace, anyspace) + (vm,) * 8,
            scratch_shapes=[
                pltpu.VMEM((32, D), F32), pltpu.VMEM((D * 3 * G, H), BF16), pltpu.VMEM((768, H), F32),
                pltpu.VMEM((D, 768), BF16), pltpu.VMEM((D, FL), BF16), pltpu.VMEM((FL, D), BF16),
                pltpu.VMEM((R0, G, S, H), BF16), pltpu.VMEM((R0, G, S, H), BF16), pltpu.VMEM((2, 128), jnp.int32),
                pltpu.VMEM((B, D), BF16), pltpu.VMEM((B, D), BF16), pltpu.VMEM((B, H), F32), pltpu.VMEM((B, H), F32),
                pltpu.VMEM((B, FL), BF16), pltpu.VMEM((G * H, 2 * CH), BF16), pltpu.VMEM((2 * CH, S), BF16), pltpu.VMEM((2 * CH, H), F32),
                pltpu.VMEM((CH, G * H), BF16), pltpu.VMEM((R0, D), F32),
                dma((19,)), dma((R0 // NG,)), dma((R0 // NG,)), dma((R0 // NG,)), dma((R0 // NG,)), dma((PER,)),
            ],
            compiler_params=pltpu.CompilerParams(vmem_limit_bytes=38 * MIB),
            name="local_part",
        )(hbm(x), *[hbm(t.reshape(1, D)) for t in (ln_attn_gamma, ln_attn_beta, ln_mlp_gamma, ln_mlp_beta)],
          hbm(wq), hbm(wo), hbm(w_up), hbm(w_down), hbm(k_cache), hbm(v_cache), positions, hbm(pos2))

        n = len(PARTS)
        block = pltpu.VMEM((NR, G, S, H), BF16)
        kblock = pltpu.VMEM((NR - CH, G, S, H), BF16)
        kpblock = pltpu.VMEM((CH, G, S, H), BF16)
        k2, v2, o = pl.pallas_call(
            reduce_kernel,
            out_shape=(kblock, block, pltpu.VMEM((B, D), BF16)),
            in_specs=[anyspace] * 2 + [vm] * 9,
            out_specs=(vm,) * 3,
            scratch_shapes=[
                pltpu.VMEM((G * H, 2 * CH), BF16), pltpu.VMEM((2 * CH, S), BF16),
                pltpu.VMEM((2 * CH, H), F32), pltpu.VMEM((CH, G * H), BF16), pltpu.VMEM((NR, D), BF16), pltpu.VMEM((B // 2, D), BF16),
                pltpu.VMEM((B // 2, D), BF16), pltpu.VMEM((3, B // 2, D // 4), BF16), pltpu.VMEM((B, D), BF16),
                dma((NR // NG - PER,)), dma((NR // NG,)),
                dma((n,)), dma((n,)), dma((n, 3)), dma((n, 3)), dma((n, 3)), dma((n, 3)), dma((n,)), dma((n,)),
            ],
            compiler_params=pltpu.CompilerParams(vmem_limit_bytes=16 * MIB, collective_id=0, has_side_effects=True),
            name="reduce_part",
        )(hbm(k_cache), hbm(v_cache), q, kn, vn, m, part, xv, wov, kp, pos2)

        _, _, _, kf, vf, out = pl.pallas_call(
            write_kernel,
            out_shape=(kpblock, kblock, block, cache, cache, jax.ShapeDtypeStruct((B, D), BF16)),
            in_specs=[vm] * 6 + [sm] + [anyspace] * 2,
            out_specs=(vm,) * 3 + (anyspace,) * 3,
            scratch_shapes=[dma((2 * (NR // NG) + 1,))],
            input_output_aliases={0: 0, 1: 1, 2: 2, 7: 3, 8: 4},
            compiler_params=pltpu.CompilerParams(vmem_limit_bytes=4 * MIB),
            name="write_part",
        )(kp, k2, v2, o, kn, vn, positions, k0, v0)
        return out, kf, vf

    return jax.shard_map(device_step, mesh=mesh, in_specs=(row_spec, vec_spec, vec_spec, vec_spec, vec_spec, P(None, 'tp', None, None), P('tp', None, None, None), P(None, 'tp'), P('tp', None), cache_spec, cache_spec, P('dp')), out_specs=(row_spec, cache_spec, cache_spec), check_vma=False)
```

time: 51.4 us -> 45.8 us (0.89)
  Pallas kernels: 50.6 us -> 45 us
    pallas_call x2, Pallas kernels: 38.1 us -> 33.1 us  [the longest x1 23.7 us: device_step(): pl.pallas_call(reduce_kernel, out_shape=(kblock, block, pltpu.VMEM((B, D)...]
    pallas_call x1, Pallas kernels: 12.5 us -> 11.9 us  [device_step(): pl.pallas_call(local_kernel, out_shape=(cache, cache) + (pltpu.VMEM((B, G...]
where the time goes in v2:
time: 45.8 us; the launch traced here: 45.7 us
  Pallas kernels  45 us (98%)
  between operations  0.67 us (1%)
    pallas_call x1, Pallas kernels, device_step(): pl.pallas_call(reduce_kernel, out_shape=(kblock, block, pltpu.VMEM((B, D)...  23.7 us
    pallas_call x1, Pallas kernels, device_step(): pl.pallas_call(local_kernel, out_shape=(cache, cache) + (pltpu.VMEM((B, G...  11.9 us
    pallas_call x1, Pallas kernels, device_step(): pl.pallas_call(write_kernel, out_shape=(kpblock, kblock, block, cache, ca...  9.43 us

profile of v2, /device:TPU:0, one launch (start us, length us, event | category | flops | bytes accessed | tf_op | source)
XLA Modules:
  0.0 45.7 jit_solution(15238293902680025436)
XLA Ops:
  0.6 0.0 copy-start
  0.6 11.9 %local_part.1 = (bf16[256,2,128,128]{3,2,1,0:T(8,128)(2,1)}, bf16[256,2,128,128]{3,2,1,0:T(8,128)(2,1)}, f32[256,256]{1,0:T(8,128)S(1)}, f32[256,256]{1,0:T(8,12...) custom-call(bf16[256,2048]{1,0:T(8,128)(2,1)} %x_h.1, ...), custom_call_target="tpu_custom_call" | custom-call | tf_op jit(solution)/shard_map/local_part/pallas_call | solution.py:484
  12.5 0.0 copy-done
  12.6 23.7 %reduce_part.1 = (bf16[128,2,128,128]{3,2,1,0:T(8,128)(2,1)S(1)}, bf16[192,2,128,128]{3,2,1,0:T(8,128)(2,1)S(1)}, bf16[256,2048]{1,0:T(8,128)(2,1)S(1)}) custom-call(bf16[256,2,128,128]{3,2,1,0:T(8,128)(2,1)} %k_h.3, bf16[256,2,128,128]{3,2,1,0:T(8,128)(2,1)} %v_h.3, f32[256,256]{1,0:T(8,128)S(1)} %get-tuple-element.20.q_i, ...), custom_call_target="tpu_custom_call" | custom-call | tf_op jit(solution)/shard_map/reduce_part/pallas_call | solution.py:508
  36.2 9.4 %write_part.1 = (bf16[64,2,128,128]{3,2,1,0:T(8,128)(2,1)S(1)}, bf16[128,2,128,128]{3,2,1,0:T(8,128)(2,1)S(1)}, bf16[192,2,128,128]{3,2,1,0:T(8,128)(2,1)S(1)}, ...) custom-call(bf16[64,2,128,128]{3,2,1,0:T(8,128)(2,1)S(1)} %get-tuple, ...), custom_call_target="tpu_custom_call", output_to_operand_aliasing={{0}: (0, {}), {1}: (1, {}), {2}: (2, {}), {3}: (7, {}), {4}... | custom-call | tf_op jit(solution)/shard_map/write_part/pallas_call | solution.py:524
Async XLA Ops:
  0.6 11.9 %copy-start = (s32[256]{0:T(256)S(1)}, s32[256]{0:T(256)}, u32[]{:S(2)}) copy-start(s32[256]{0:T(256)} %pos_s.3) | copy-start | bytes 3076

commit v3 on v2

--- a/solution.py
+++ b/solution.py
@@ -45,8 +45,12 @@
     qt_ref[pl.ds(H, H), :] = jnp.where(low, 0.0, turned).astype(BF16)
 
 
+def aligned(row):
+    return pl.ds(row if isinstance(row, int) else pl.multiple_of(row, NG), NG)
+
+
 def add_rows(buf, new_ref, pos_s, row, at):
-    rows = pl.ds(row if isinstance(row, int) else pl.multiple_of(row, NG), NG)
+    rows = aligned(row)
     new = [new_ref[rows, pl.ds(g * H, H)] for g in range(G)]
     inside = iota((NG, H), 0).astype(F32).astype(BF16)
     for u in range(NG):
@@ -66,7 +70,7 @@
     return acc
 
 
-def attend_scores(c, at, wait, also, kbuf, q_ref, kn_ref, pos_v, qt_v, p_v, pn_v):
+def attend_scores(c, at, wait, also, kbuf, q_ref, kn_ref, pos_v, qt_v, p_v, pn_v, between=None):
     build_queries(q_ref, c * CH, qt_v)
     rows = pl.ds(c * CH, CH)
     with_new = jnp.concatenate([q_ref[rows, pl.ds(g * H, H)] * kn_ref[rows, pl.ds(g * H, H)] for g in range(G)], axis=0)
@@ -82,7 +86,14 @@
             also(i)
         return acc
 
-    acc = lax.fori_loop(0, CH // NG // GI, step, jnp.zeros((S, 2 * CH), F32))
+    acc = jnp.zeros((S, 2 * CH), F32)
+    if between is None:
+        acc = lax.fori_loop(0, PER // GI, step, acc)
+    else:
+        for j in range(PER // GI):
+            acc = step(j, acc)
+            if j == 0:
+                between()
     slot = iota((S, 2 * CH), 0)
     s = jnp.where(slot < new_at, acc * SCALE, jnp.where(slot == new_at, s_new * SCALE, NEG_BIG))
     p = softmax_slots(s).astype(BF16).astype(F32)
@@ -91,19 +102,26 @@
     pn_v[...] = jnp.broadcast_to(p_new, (2 * CH, H)).T
 
 
-def attend_context(c, at, lo, hi, wait, also, vbuf, vn_ref, p_v, pn_v, ctx_v):
-    @pl.loop(0, (hi - lo) // GI)
-    def _(j):
+def attend_context(c, at, lo, hi, wait, also, vbuf, vn_ref, p_v, pn_v, ctx_v, between=None):
+    def step(j):
         for w in range(GI):
             wait(lo + j * GI + w)
         for w in range(GI):
             i = lo + j * GI + w
             ctx = context_of_group(vbuf, p_v, at + i * NG, i * NG)
-            rows = pl.ds(pl.multiple_of(c * CH + i * NG, NG), NG)
+            rows = aligned(c * CH + i * NG)
             for g in range(G):
-                new = pn_v[pl.ds(pl.multiple_of(g * CH + i * NG, NG), NG), :] * vn_ref[rows, pl.ds(g * H, H)]
-                ctx_v[pl.ds(pl.multiple_of(i * NG, NG), NG), pl.ds(g * H, H)] = (ctx[g] + new).astype(BF16)
+                new = pn_v[aligned(g * CH + i * NG), :] * vn_ref[rows, pl.ds(g * H, H)]
+                ctx_v[aligned(i * NG), pl.ds(g * H, H)] = (ctx[g] + new).astype(BF16)
             also(i)
+
+    if between is None:
+        pl.loop(0, (hi - lo) // GI)(step)
+    else:
+        for j in range((hi - lo) // GI):
+            step(j)
+            if j == 0:
+                between()
 
 
 def pos_columns(pos_v, chunk):
@@ -123,7 +141,7 @@
     zero = jnp.zeros((NG, S), BF16)
     total = []
     for g in range(G):
-        probs = p_ref[pl.ds(pl.multiple_of(g * CH + local, NG), NG), :]
+        probs = p_ref[aligned(g * CH + local), :]
         tot = None
         for u in range(0, NG, 2):
             ps = [jnp.where(rows16 == jnp.asarray(u + w, BF16), probs, zero) for w in range(2)]
@@ -263,13 +281,14 @@
         u = dot(min_v[...], wu_v[:, pl.ds(256 * n, 256)])
         h_v[:, pl.ds(256 * n, 256)] = (0.5 * u * (1.0 + lax.erf(u * (2.0 ** -0.5)))).astype(BF16)
         add_rows(vb, vn_o, pos_s, R0 - CH + n * NG, R0 - CH + n * NG)
-    for j in range(PER):
-        kcopy(R0 // NG - PER + j, vb, vo_h, sem_vo).start()
     for c in c_wd:
         c.wait()
     for n in range(8):
         cs = pl.ds(256 * n, 256)
         m_o[:, cs] = dot(h_v[...], wd_v[:, cs])
+        if n == 0:
+            for j in range(PER):
+                kcopy(R0 // NG - PER + j, vb, vo_h, sem_vo).start()
         part_o[:, cs] = (a_v[:, cs] + m_o[pl.ds(0, R0), cs]).astype(BF16)
 
     for cp in kp_copies:
@@ -308,7 +327,6 @@
             vcopy((c - first) * per + i).start()
 
     issue_v(1)
-    issue_k(2)
 
     sib = tp + 1 - 2 * core
     peers = []
@@ -378,16 +396,16 @@
     def nothing(i):
         pass
 
-    def scores(c):
+    def scores(c, between):
         if c == first:
-            attend_scores(c, 0, nothing, nothing, kp_i, q_i, kn_i, pos_i, qt_v, p_v, pn_v)
+            attend_scores(c, 0, nothing, nothing, kp_i, q_i, kn_i, pos_i, qt_v, p_v, pn_v, between)
         else:
             at = (c - first - 1) * per
-            attend_scores(c, at * NG, lambda i: kcopy(at + i).wait(), nothing, k2, q_i, kn_i, pos_i, qt_v, p_v, pn_v)
-
-    def context(c, lo, hi):
+            attend_scores(c, at * NG, lambda i: kcopy(at + i).wait(), nothing, k2, q_i, kn_i, pos_i, qt_v, p_v, pn_v, between)
+
+    def context(c, lo, hi, between):
         at = (c - first) * CH
-        attend_context(c, at, lo, hi, lambda i: vcopy((c - first) * per + i).wait(), nothing, v2, vn_i, p_v, pn_v, ctx_v)
+        attend_context(c, at, lo, hi, lambda i: vcopy((c - first) * per + i).wait(), nothing, v2, vn_i, p_v, pn_v, ctx_v, between)
         n = (hi - lo) * NG
         for k in range(8):
             cs = pl.ds(256 * k, 256)
@@ -396,32 +414,49 @@
 
     pl.semaphore_wait(barrier, 4)
     step_a(0)
-    scores(1)
+    def between1():
+        issue_k(2)
+
+    scores(1, between1)
     step_b(0)
-    issue_v(2)
-    context(1, 0, per)
+    def between2():
+        issue_v(2)
+
+    context(1, 0, per, between2)
     step_a(1)
-    issue_k(3)
-    scores(2)
+    def between3():
+        issue_k(3)
+
+    scores(2, between3)
     step_b(1)
+    def between4():
+        issue_v(3)
+
+    context(2, 0, per, between4)
+    step_a(2)
+    def between5():
+        step_b(2)
+
+    scores(3, between5)
     step_c(0)
-    issue_v(3)
-    context(2, 0, per)
-    step_a(2)
-    scores(3)
-    step_b(2)
-    context(3, 0, per // 2)
+    def between6():
+        pass
+
+    context(3, 0, per // 2, between6)
     step_a(3)
-    step_c(1)
-    context(3, per // 2, per)
+    def between7():
+        pass
+
+    context(3, per // 2, per, between7)
     step_a(4)
     step_b(3)
     step_b(4)
-    step_d(0)
+    step_c(1)
     step_c(2)
-    step_d(1)
     step_c(3)
     step_c(4)
+    step_d(0)
+    step_d(1)
     step_d(2)
     step_d(3)
     step_d(4)
@@ -443,23 +478,25 @@
     def copy(src, dst, i, k):
         return pltpu.make_async_copy(src.at[pl.ds(NG * i, NG)], dst.at[pl.ds(R0 + NG * k, NG)], sem.at[k if dst is ko_h else n + k])
 
+    late = None
     for src, dst, new, first, count in ((kp3, ko_h, kn_i, 0, PER), (v3, vo_h, vn_i, 0, n), (k3, ko_h, kn_i, PER, n - PER)):
-        @pl.loop(0, count)
+        add_rows(src, new, pos_s, R0 + first * NG, 0)
+        if late is not None:
+            late.start()
+
+        @pl.loop(1, count)
         def _(i, src=src, dst=dst, new=new, first=first):
             add_rows(src, new, pos_s, R0 + (first + i) * NG, i * NG)
-
-            @pl.when(i > 0)
-            def _():
-                copy(src, dst, i - 1, first + i - 1).start()
-
-        copy(src, dst, count - 1, first + count - 1).start()
+            copy(src, dst, i - 1, first + i - 1).start()
+
+        late = copy(src, dst, count - 1, first + count - 1)
+    c_out.wait()
+    late.start()
 
     for src, dst, first, count in ((kp3, ko_h, 0, PER), (v3, vo_h, 0, n), (k3, ko_h, PER, n - PER)):
         @pl.loop(0, count)
         def _(i, src=src, dst=dst, first=first):
             copy(src, dst, i, first + i).wait()
-
-    c_out.wait()
 
 
 def solution(mesh):

time: 45.8 us -> 45.4 us (level)
  Pallas kernels: 45 us -> 44.5 us
    pallas_call x1, Pallas kernels: 23.7 us -> 23 us  [device_step(): pl.pallas_call(reduce_kernel, out_shape=(kblock, block, pltpu.VMEM((B, D)...]
where the time goes in v3:
time: 45.4 us; the launch traced here: 45.3 us
  Pallas kernels  44.5 us (98%)
  between operations  0.83 us (2%)
    pallas_call x1, Pallas kernels, device_step(): pl.pallas_call(reduce_kernel, out_shape=(kblock, block, pltpu.VMEM((B, D)...  23 us
    pallas_call x1, Pallas kernels, device_step(): pl.pallas_call(local_kernel, out_shape=(cache, cache) + (pltpu.VMEM((B, G...  12 us
    pallas_call x1, Pallas kernels, device_step(): pl.pallas_call(write_kernel, out_shape=(kpblock, kblock, block, cache, ca...  9.43 us

profile of v3, /device:TPU:0, one launch (start us, length us, event | category | flops | bytes accessed | tf_op | source)
XLA Modules:
  0.0 45.3 jit_solution(8256599277153351176)
XLA Ops:
  0.6 0.0 copy-start
  0.6 12.0 %local_part.1 = (bf16[256,2,128,128]{3,2,1,0:T(8,128)(2,1)}, bf16[256,2,128,128]{3,2,1,0:T(8,128)(2,1)}, f32[256,256]{1,0:T(8,128)S(1)}, f32[256,256]{1,0:T(8,12...) custom-call(bf16[256,2048]{1,0:T(8,128)(2,1)} %x_h.1, ...), custom_call_target="tpu_custom_call" | custom-call | tf_op jit(solution)/shard_map/local_part/pallas_call | solution.py:521
  12.7 0.0 copy-done
  12.7 23.0 %reduce_part.1 = (bf16[128,2,128,128]{3,2,1,0:T(8,128)(2,1)S(1)}, bf16[192,2,128,128]{3,2,1,0:T(8,128)(2,1)S(1)}, bf16[256,2048]{1,0:T(8,128)(2,1)S(1)}) custom-call(bf16[256,2,128,128]{3,2,1,0:T(8,128)(2,1)} %k_h.3, bf16[256,2,128,128]{3,2,1,0:T(8,128)(2,1)} %v_h.3, f32[256,256]{1,0:T(8,128)S(1)} %get-tuple-element.20.q_i, ...), custom_call_target="tpu_custom_call" | custom-call | tf_op jit(solution)/shard_map/reduce_part/pallas_call | solution.py:545
  35.7 9.4 %write_part.1 = (bf16[64,2,128,128]{3,2,1,0:T(8,128)(2,1)S(1)}, bf16[128,2,128,128]{3,2,1,0:T(8,128)(2,1)S(1)}, bf16[192,2,128,128]{3,2,1,0:T(8,128)(2,1)S(1)}, ...) custom-call(bf16[64,2,128,128]{3,2,1,0:T(8,128)(2,1)S(1)} %get-tuple, ...), custom_call_target="tpu_custom_call", output_to_operand_aliasing={{0}: (0, {}), {1}: (1, {}), {2}: (2, {}), {3}: (7, {}), {4}... | custom-call | tf_op jit(solution)/shard_map/write_part/pallas_call | solution.py:561
Async XLA Ops:
  0.6 12.0 %copy-start = (s32[256]{0:T(256)S(1)}, s32[256]{0:T(256)}, u32[]{:S(2)}) copy-start(s32[256]{0:T(256)} %pos_s.3) | copy-start | bytes 3076

commit v4 on v3

--- a/solution.py
+++ b/solution.py
@@ -280,15 +280,15 @@
     for n in range(4):
         u = dot(min_v[...], wu_v[:, pl.ds(256 * n, 256)])
         h_v[:, pl.ds(256 * n, 256)] = (0.5 * u * (1.0 + lax.erf(u * (2.0 ** -0.5)))).astype(BF16)
-        add_rows(vb, vn_o, pos_s, R0 - CH + n * NG, R0 - CH + n * NG)
+        for i in ((0, 1), (2,), (3,), ())[n]:
+            add_rows(vb, vn_o, pos_s, R0 - CH + i * NG, R0 - CH + i * NG)
+    for j in range(PER):
+        kcopy(R0 // NG - PER + j, vb, vo_h, sem_vo).start()
     for c in c_wd:
         c.wait()
     for n in range(8):
         cs = pl.ds(256 * n, 256)
         m_o[:, cs] = dot(h_v[...], wd_v[:, cs])
-        if n == 0:
-            for j in range(PER):
-                kcopy(R0 // NG - PER + j, vb, vo_h, sem_vo).start()
         part_o[:, cs] = (a_v[:, cs] + m_o[pl.ds(0, R0), cs]).astype(BF16)
 
     for cp in kp_copies:
@@ -490,13 +490,14 @@
             copy(src, dst, i - 1, first + i - 1).start()
 
         late = copy(src, dst, count - 1, first + count - 1)
-    c_out.wait()
     late.start()
 
     for src, dst, first, count in ((kp3, ko_h, 0, PER), (v3, vo_h, 0, n), (k3, ko_h, PER, n - PER)):
         @pl.loop(0, count)
         def _(i, src=src, dst=dst, first=first):
             copy(src, dst, i, first + i).wait()
+
+    c_out.wait()
 
 
 def solution(mesh):

time: 45.4 us -> 45.1 us (level)
  no operation moved by 1% of the time
where the time goes in v4:
time: 45.1 us; the launch traced here: 45 us
  Pallas kernels  44.3 us (98%)
  between operations  0.67 us (1%)
    pallas_call x1, Pallas kernels, device_step(): pl.pallas_call(reduce_kernel, out_shape=(kblock, block, pltpu.VMEM((B, D)...  23 us
    pallas_call x1, Pallas kernels, device_step(): pl.pallas_call(local_kernel, out_shape=(cache, cache) + (pltpu.VMEM((B, G...  11.9 us
    pallas_call x1, Pallas kernels, device_step(): pl.pallas_call(write_kernel, out_shape=(kpblock, kblock, block, cache, ca...  9.43 us

profile of v4, /device:TPU:0, one launch (start us, length us, event | category | flops | bytes accessed | tf_op | source)
XLA Modules:
  0.0 45.0 jit_solution(17779854817796530842)
XLA Ops:
  0.6 0.0 copy-start
  0.6 11.9 %local_part.1 = (bf16[256,2,128,128]{3,2,1,0:T(8,128)(2,1)}, bf16[256,2,128,128]{3,2,1,0:T(8,128)(2,1)}, f32[256,256]{1,0:T(8,128)S(1)}, f32[256,256]{1,0:T(8,12...) custom-call(bf16[256,2048]{1,0:T(8,128)(2,1)} %x_h.1, ...), custom_call_target="tpu_custom_call" | custom-call | tf_op jit(solution)/shard_map/local_part/pallas_call | solution.py:522
  12.5 0.0 copy-done
  12.5 23.0 %reduce_part.1 = (bf16[128,2,128,128]{3,2,1,0:T(8,128)(2,1)S(1)}, bf16[192,2,128,128]{3,2,1,0:T(8,128)(2,1)S(1)}, bf16[256,2048]{1,0:T(8,128)(2,1)S(1)}) custom-call(bf16[256,2,128,128]{3,2,1,0:T(8,128)(2,1)} %k_h.3, bf16[256,2,128,128]{3,2,1,0:T(8,128)(2,1)} %v_h.3, f32[256,256]{1,0:T(8,128)S(1)} %get-tuple-element.20.q_i, ...), custom_call_target="tpu_custom_call" | custom-call | tf_op jit(solution)/shard_map/reduce_part/pallas_call | solution.py:546
  35.5 9.4 %write_part.1 = (bf16[64,2,128,128]{3,2,1,0:T(8,128)(2,1)S(1)}, bf16[128,2,128,128]{3,2,1,0:T(8,128)(2,1)S(1)}, bf16[192,2,128,128]{3,2,1,0:T(8,128)(2,1)S(1)}, ...) custom-call(bf16[64,2,128,128]{3,2,1,0:T(8,128)(2,1)S(1)} %get-tuple, ...), custom_call_target="tpu_custom_call", output_to_operand_aliasing={{0}: (0, {}), {1}: (1, {}), {2}: (2, {}), {3}: (7, {}), {4}... | custom-call | tf_op jit(solution)/shard_map/write_part/pallas_call | solution.py:562
Async XLA Ops:
  0.6 11.9 %copy-start = (s32[256]{0:T(256)S(1)}, s32[256]{0:T(256)}, u32[]{:S(2)}) copy-start(s32[256]{0:T(256)} %pos_s.3) | copy-start | bytes 3076

commit v5 on v4

--- a/solution.py
+++ b/solution.py
@@ -303,7 +303,7 @@
 
 def reduce_kernel(k_h, v_h, q_i, kn_i, vn_i, m_i, part_i, x_v, wo_v, kp_i, pos_i,
                   k2, v2, out_o,
-                  qt_v, p_v, pn_v, ctx_v, part_v, d2_v, sum_v, rs_v, gat_v,
+                  qt_v, p_v, pn_v, ctx_v, part_v, d2_v, sum_v, rs_v,
                   sem_k, sem_v, s_d, r_d, s_rs, r_rs, s_ag, r_ag, s_e, r_e):
     tp = lax.axis_index("tp")
     core = tp % 2
@@ -330,7 +330,7 @@
 
     sib = tp + 1 - 2 * core
     peers = []
-    for k in range(1, 4):
+    for k in (3, 2, 1):
         chip_k = (chip // 2 + k // 2) % 2 * 2 + (chip % 2 + k % 2) % 2
         peers.append((chip_k, chip_k * 2 + core))
 
@@ -363,11 +363,11 @@
                 for k, (ck, t) in enumerate(peers)]
 
     def c_copies(c):
-        piece = gat_v.at[out_rows(c), my_cols]
+        piece = out_o.at[out_rows(c), my_cols]
         return [remote(piece, piece, s_ag.at[c, k], r_ag.at[c, k], t) for k, (_, t) in enumerate(peers)]
 
     def d_copy(c):
-        rows = gat_v.at[out_rows(c)]
+        rows = out_o.at[out_rows(c)]
         return remote(rows, rows, s_e.at[c], r_e.at[c], sib)
 
     def step_a(c):
@@ -384,7 +384,7 @@
         for k, cp in enumerate(b_copies(c)):
             cp.wait_recv()
             tot = tot + rs_v[k, half(c)].astype(F32)
-        gat_v[out_rows(c), my_cols] = tot.astype(BF16)
+        out_o[out_rows(c), my_cols] = tot.astype(BF16)
         for cp in c_copies(c):
             cp.start()
 
@@ -467,7 +467,6 @@
         for cp in c_copies(c):
             cp.wait_send()
         d_copy(c).wait()
-    out_o[...] = gat_v[...]
 
 
 def write_kernel(kp_i, k_i, v_i, o_i, kn_i, vn_i, pos_s, k0_h, v0_h, kp3, k3, v3, ko_h, vo_h, o_h, sem):
@@ -551,7 +550,7 @@
             scratch_shapes=[
                 pltpu.VMEM((G * H, 2 * CH), BF16), pltpu.VMEM((2 * CH, S), BF16),
                 pltpu.VMEM((2 * CH, H), F32), pltpu.VMEM((CH, G * H), BF16), pltpu.VMEM((NR, D), BF16), pltpu.VMEM((B // 2, D), BF16),
-                pltpu.VMEM((B // 2, D), BF16), pltpu.VMEM((3, B // 2, D // 4), BF16), pltpu.VMEM((B, D), BF16),
+                pltpu.VMEM((B // 2, D), BF16), pltpu.VMEM((3, B // 2, D // 4), BF16),
                 dma((NR // NG - PER,)), dma((NR // NG,)),
                 dma((n,)), dma((n,)), dma((n, 3)), dma((n, 3)), dma((n, 3)), dma((n, 3)), dma((n,)), dma((n,)),
             ],

time: 45.1 us -> 44.8 us (level)
  no operation moved by 1% of the time
where the time goes in v5:
time: 44.8 us; the launch traced here: 44.7 us
  Pallas kernels  44 us (98%)
  between operations  0.67 us (1%)
    pallas_call x1, Pallas kernels, device_step(): pl.pallas_call(reduce_kernel, out_shape=(kblock, block, pltpu.VMEM((B, D)...  22.7 us
    pallas_call x1, Pallas kernels, device_step(): pl.pallas_call(local_kernel, out_shape=(cache, cache) + (pltpu.VMEM((B, G...  11.9 us
    pallas_call x1, Pallas kernels, device_step(): pl.pallas_call(write_kernel, out_shape=(kpblock, kblock, block, cache, ca...  9.43 us

profile of v5, /device:TPU:0, one launch (start us, length us, event | category | flops | bytes accessed | tf_op | source)
XLA Modules:
  0.0 44.7 jit_solution(15724221011571353909)
XLA Ops:
  0.6 0.0 copy-start
  0.6 11.9 %local_part.1 = (bf16[256,2,128,128]{3,2,1,0:T(8,128)(2,1)}, bf16[256,2,128,128]{3,2,1,0:T(8,128)(2,1)}, f32[256,256]{1,0:T(8,128)S(1)}, f32[256,256]{1,0:T(8,12...) custom-call(bf16[256,2048]{1,0:T(8,128)(2,1)} %x_h.1, ...), custom_call_target="tpu_custom_call" | custom-call | tf_op jit(solution)/shard_map/local_part/pallas_call | solution.py:521
  12.5 0.0 copy-done
  12.6 22.7 %reduce_part.1 = (bf16[128,2,128,128]{3,2,1,0:T(8,128)(2,1)S(1)}, bf16[192,2,128,128]{3,2,1,0:T(8,128)(2,1)S(1)}, bf16[256,2048]{1,0:T(8,128)(2,1)S(1)}) custom-call(bf16[256,2,128,128]{3,2,1,0:T(8,128)(2,1)} %k_h.3, bf16[256,2,128,128]{3,2,1,0:T(8,128)(2,1)} %v_h.3, f32[256,256]{1,0:T(8,128)S(1)} %get-tuple-element.20.q_i, ...), custom_call_target="tpu_custom_call" | custom-call | tf_op jit(solution)/shard_map/reduce_part/pallas_call | solution.py:545
  35.3 9.4 %write_part.1 = (bf16[64,2,128,128]{3,2,1,0:T(8,128)(2,1)S(1)}, bf16[128,2,128,128]{3,2,1,0:T(8,128)(2,1)S(1)}, bf16[192,2,128,128]{3,2,1,0:T(8,128)(2,1)S(1)}, ...) custom-call(bf16[64,2,128,128]{3,2,1,0:T(8,128)(2,1)S(1)} %get-tuple, ...), custom_call_target="tpu_custom_call", output_to_operand_aliasing={{0}: (0, {}), {1}: (1, {}), {2}: (2, {}), {3}: (7, {}), {4}... | custom-call | tf_op jit(solution)/shard_map/write_part/pallas_call | solution.py:561
Async XLA Ops:
  0.6 11.9 %copy-start = (s32[256]{0:T(256)S(1)}, s32[256]{0:T(256)}, u32[]{:S(2)}) copy-start(s32[256]{0:T(256)} %pos_s.3) | copy-start | bytes 3076

commit v6 on v5

--- a/solution.py
+++ b/solution.py
@@ -434,11 +434,11 @@
 
     context(2, 0, per, between4)
     step_a(2)
+    step_c(0)
     def between5():
         step_b(2)
 
     scores(3, between5)
-    step_c(0)
     def between6():
         pass
 

time: 44.8 us -> 44.6 us (level)
  no operation moved by 1% of the time
where the time goes in v6:
time: 44.6 us; the launch traced here: 44.4 us
  Pallas kernels  43.8 us (98%)
  between operations  0.67 us (2%)
    pallas_call x1, Pallas kernels, device_step(): pl.pallas_call(reduce_kernel, out_shape=(kblock, block, pltpu.VMEM((B, D)...  22.5 us
    pallas_call x1, Pallas kernels, device_step(): pl.pallas_call(local_kernel, out_shape=(cache, cache) + (pltpu.VMEM((B, G...  11.9 us
    pallas_call x1, Pallas kernels, device_step(): pl.pallas_call(write_kernel, out_shape=(kpblock, kblock, block, cache, ca...  9.43 us

profile of v6, /device:TPU:0, one launch (start us, length us, event | category | flops | bytes accessed | tf_op | source)
XLA Modules:
  0.0 44.4 jit_solution(453982755300800742)
XLA Ops:
  0.6 0.0 copy-start
  0.6 11.9 %local_part.1 = (bf16[256,2,128,128]{3,2,1,0:T(8,128)(2,1)}, bf16[256,2,128,128]{3,2,1,0:T(8,128)(2,1)}, f32[256,256]{1,0:T(8,128)S(1)}, f32[256,256]{1,0:T(8,12...) custom-call(bf16[256,2048]{1,0:T(8,128)(2,1)} %x_h.1, ...), custom_call_target="tpu_custom_call" | custom-call | tf_op jit(solution)/shard_map/local_part/pallas_call | solution.py:521
  12.5 0.0 copy-done
  12.5 22.5 %reduce_part.1 = (bf16[128,2,128,128]{3,2,1,0:T(8,128)(2,1)S(1)}, bf16[192,2,128,128]{3,2,1,0:T(8,128)(2,1)S(1)}, bf16[256,2048]{1,0:T(8,128)(2,1)S(1)}) custom-call(bf16[256,2,128,128]{3,2,1,0:T(8,128)(2,1)} %k_h.3, bf16[256,2,128,128]{3,2,1,0:T(8,128)(2,1)} %v_h.3, f32[256,256]{1,0:T(8,128)S(1)} %get-tuple-element.20.q_i, ...), custom_call_target="tpu_custom_call" | custom-call | tf_op jit(solution)/shard_map/reduce_part/pallas_call | solution.py:545
  35.0 9.4 %write_part.1 = (bf16[64,2,128,128]{3,2,1,0:T(8,128)(2,1)S(1)}, bf16[128,2,128,128]{3,2,1,0:T(8,128)(2,1)S(1)}, bf16[192,2,128,128]{3,2,1,0:T(8,128)(2,1)S(1)}, ...) custom-call(bf16[64,2,128,128]{3,2,1,0:T(8,128)(2,1)S(1)} %get-tuple, ...), custom_call_target="tpu_custom_call", output_to_operand_aliasing={{0}: (0, {}), {1}: (1, {}), {2}: (2, {}), {3}: (7, {}), {4}... | custom-call | tf_op jit(solution)/shard_map/write_part/pallas_call | solution.py:561
Async XLA Ops:
  0.6 11.9 %copy-start = (s32[256]{0:T(256)S(1)}, s32[256]{0:T(256)}, u32[]{:S(2)}) copy-start(s32[256]{0:T(256)} %pos_s.3) | copy-start | bytes 3076
